TPU v7x, 256 devices: a whole 4x4x8 slice. The times are simulated.
256 devices in a mesh: gx: 16 (over y_hi, x, core), gy: 8 (over z), gz: 2 (over y_lo).
Axes of the slice: x: 4, y: 4 (y_hi: 2, y_lo: 2; y = y_hi * 2 + y_lo), z: 8, core: 2. Of those that a mesh axis runs over, the one named last changes fastest.
Arguments:
- particles: float32 [32768, 512], P(('gx', 'gy', 'gz')), may hold values from -6 to 6
- scores: bfloat16 [32768, 512], P(('gx', 'gy', 'gz')), may hold values from -6 to 6
- band_power: int32 [512], replicated, may hold values from 7 to 8
Outputs:
- drift: float32 [32768, 512], P(('gx', 'gy', 'gz'))
All inputs are finite; a program needn't handle non-finite values.
Results may differ from a plain program's by a relative error of at most 0.0046.
Values may be sent and summed in bfloat16 or wider, within the bound.
A program may use at most 64 MiB of HBM per device.

v0:
```python
import jax
import jax.numpy as jnp
from jax import lax
from jax.sharding import Mesh
from jax.sharding import PartitionSpec as P

GX = ("gx_0", "gx_1", "gx_2")
GX_GY_GZ = ("gx_0", "gx_1", "gx_2", "gy", "gz")


def sent_to_all(value, axis):
    copies = jnp.broadcast_to(value, (lax.axis_size(axis), *value.shape))
    return lax.all_to_all(copies, axis, split_axis=0, concat_axis=0, tiled=True)


def in_order(tiles, dim):
    shape = list(tiles.shape[1:])
    shape[dim] *= tiles.shape[0]
    return jnp.moveaxis(tiles, 0, dim).reshape(shape)


def gather_axes(value, axes, dim):
    far, near = axes
    leading = sent_to_all(value, far)
    tiles = jnp.swapaxes(sent_to_all(leading, near), 0, 1)
    return in_order(tiles.reshape(-1, *value.shape), dim)


def side_by_side(arrays, axis, dim, along):
    widths = [a.shape[along] for a in arrays]
    both = jnp.concatenate(arrays, axis=along)
    result = lax.all_gather(both, axis, axis=dim, tiled=True)
    return tuple(jnp.split(result, [sum(widths[:k]) for k in range(1, len(widths))], axis=along))


def in_blocks(value, dim, size):
    shape = value.shape
    tiles = value.reshape(*shape[:dim], size, shape[dim] // size, *shape[dim + 1 :])
    return jnp.moveaxis(tiles, dim, 0)


def summed_on_arrival(value, axis, dim):
    tiles = in_blocks(value, dim, lax.axis_size(axis))
    arrived = lax.all_to_all(tiles, axis, split_axis=0, concat_axis=0, tiled=True)
    return arrived.astype(jnp.float32).sum(axis=0)


def sum_by_axis(value, axes, dim):
    far, near = axes
    tiles = in_blocks(value, dim, lax.axis_size(far))
    nearer = summed_on_arrival(tiles, near, dim + 1)
    arrived = lax.all_to_all(
        nearer.astype(jnp.bfloat16), far, split_axis=0, concat_axis=0, tiled=True
    )
    return arrived.astype(jnp.float32).sum(axis=0)


def kernel_terms(target_rows, sources, stacked, source_squares, weights):
    target_float = target_rows.astype(jnp.float32)
    target_squares = jnp.sum(jnp.square(target_float) * weights[None, :], axis=1)
    scaled = (target_float * weights[None, :]).astype(jnp.bfloat16)
    inner = lax.dot_general(
        scaled, sources, (((1,), (1,)), ((), ())), preferred_element_type=jnp.float32
    )
    distance = target_squares[:, None] + source_squares[None, :] - 2.0 * inner
    kernel = jnp.exp(-distance).astype(jnp.bfloat16)
    products = jnp.dot(kernel, stacked, preferred_element_type=jnp.float32)
    totals = jnp.sum(kernel.astype(jnp.float32), axis=1)
    width = target_rows.shape[1]
    return products[:, :width] + 2.0 * weights[None, :] * (
        target_float * totals[:, None] - products[:, width:]
    )


def make_terms(targets, sources, source_scores, weights):
    source_squares = jnp.sum(jnp.square(sources.astype(jnp.float32)) * weights[None, :], axis=1)
    stacked = jnp.concatenate([source_scores, sources], axis=1)
    width = targets.shape[1]

    def term_rows(start, count):
        block_rows = 512
        target_blocks = targets.reshape(count // block_rows, block_rows, width)

        def one_block(target_rows):
            return kernel_terms(target_rows, sources, stacked, source_squares, weights)

        return lax.map(one_block, target_blocks).reshape(count, width)

    return term_rows


def local(particles, scores, band_power):
    weights = jnp.exp2(-band_power.astype(jnp.float32))
    rounded = particles.astype(jnp.bfloat16)
    own_rows = rounded.shape[0]
    targets = gather_axes(rounded, (("gx_0", "gx_1"), "gx_2"), 0)
    sources, source_scores = side_by_side((rounded, scores), ("gy", "gz"), 0, 1)
    term_rows = make_terms(targets, sources, source_scores, weights)
    drift = sum_by_axis(
        term_rows(jnp.int32(0), own_rows * lax.axis_size(GX)).astype(jnp.bfloat16),
        (("gx_0", "gx_1"), "gx_2"),
        0,
    )
    return drift


def solution(mesh):
    split = Mesh(
        mesh.devices.reshape(2, 4, 2, mesh.shape["gy"], mesh.shape["gz"]),
        ("gx_0", "gx_1", "gx_2", "gy", "gz"),
    )
    placed = (P(GX_GY_GZ, None), P(GX_GY_GZ, None), P())
    return jax.shard_map(
        local, mesh=split, in_specs=placed, out_specs=P(GX_GY_GZ, None), check_vma=False
    )
```

profile of v0, /device:TPU:1, one launch (start us, length us, event | category | flops | bytes accessed | tf_op | source)
XLA Modules:
  0.0 195.7 jit_solution(7415680940413923263)
XLA Ops:
  7.5 1.6 pad_maximum_fusion.1
  9.2 1.2 broadcast_in_dim.10
  10.3 7.5 %all-to-all-start = ((bf16[8,128,512]{2,1,0:T(8,128)(2,1)}), bf16[8,128,512]{2,1,0:T(8,128)(2,1)S(1)}, u32[]{:S(2)}, u32[]{:S(2)}) async-start(bf16[8,128,512]{2,1,0:T(8,128)(2,1)} %broadcast_in_dim.10), calls=%async_computation | async-start | bytes 2097152 | tf_op jit(solution)/shard_map/all_to_all | solution.py:13
  17.8 18.1 %all-to-all-done = bf16[8,128,512]{2,1,0:T(8,128)(2,1)S(1)} async-done(((bf16[8,128,512]{2,1,0:T(8,128)(2,1)}), bf16[8,128,512]{2,1,0:T(8,128)(2,1)S(1)}, u32[]{:S(2)}, u32[]{:S(2)}) %all-to-all-start) | async-done | bytes 1048608 | tf_op jit(solution)/shard_map/all_to_all | solution.py:13
  36.1 6.1 %all_to_all.20 = bf16[2,8,128,512]{3,2,1,0:T(8,128)(2,1)S(1)} all-to-all(bf16[2,8,128,512]{3,2,1,0:T(8,128)(2,1)S(1)} %broadcast_in_dim.22), channel_id=1, replica_groups=mesh['gx_0'=2,'gx_1'=4,'gx_2'=2,'gy'=8,'gz'=2] {'gx_2'}, dimensions={0} | all-to-all | bytes 4194304 | tf_op jit(solution)/shard_map/all_to_all | solution.py:13
  42.5 79.1 %all-gather.2.cloned.1.call-done = bf16[2048,1024]{1,0:T(8,128)(2,1)} async-done(((bf16[128,1024]{1,0:T(8,128)(2,1)}), bf16[2048,1024]{1,0:T(8,128)(2,1)}) %all-gather.2.cloned.1.call-update) | async-done | bytes 4194320 | tf_op jit(solution)/shard_map/all_gather | solution.py:32
  121.5 2.5 %fusion.13 = (bf16[2048,512]{1,0:T(8,128)(2,1)S(1)}, bf16[2048,512]{1,0:T(8,128)(2,1)S(1)}) fusion(bf16[2048,1024]{1,0:T(8,128)(2,1)} %all-gather.2.cloned.1.call-done), kind=kLoop, calls=%fused_computation.23 | loop fusion | bytes 8388608 | tf_op jit(solution)/shard_map/split | solution.py:33
  124.0 2.8 %pad_maximum_fusion = bf16[2048,1024]{1,0:T(8,128)(2,1)} fusion(bf16[2048,512]{1,0:T(8,128)(2,1)S(1)} %get-tuple-element.113, bf16[2048,512]{1,0:T(8,128)(2,1)S(1)} %get-tuple-element.59), kind=kLoop, calls=%fused_computation.18 | loop fusion | flops 8388608 | bytes 8388608 | tf_op jit(solution)/shard_map/concatenate | solution.py:77
  127.2 1.3 copy-done
  129.1 27.8 %while.10 = (s32[]{:T(128)}, bf16[4,512,512]{2,1,0:T(8,128)(2,1)}, bf16[4,512,512]{2,1,0:T(8,128)(2,1)S(1)}, f32[512]{0:T(512)S(1)}, f32[2048]{0:T(1024)S(1)}, /...) while((s32[]{:T(128)}, bf16[4,512,512]{2,1,0:T(8,128)(2,1)}, ...), condition=%wide.region_4.5_spmd, body=%wide.region_1.4_spmd.sunk | while | flops 3231710720 | bytes 34105976 | solution.py:87
  129.3 3.3 %convert_reduce_fusion.3 = (f32[512]{0:T(512)S(1)}, bf16[512,2048]{1,0:T(8,128)(2,1)S(1)}) fusion(bf16[2048,512]{1,0:T(8,128)(2,1)} %get-tuple-element.129, f32[512]{0:T(512)S(1)} %get-tuple-element.127, bf16[4,512,512]{2,1,0:T(8,128)(2,1)S(1)} %get-tuple-element.126, s32[]{:T(128)} %get-tuple-element.116, f32[2048]{0:T(1024)S(1)} %get-tuple-element.128, ...), kind=kOutput, calls=%fused_computation.clone.1 | convolution fusion | flops 1081867776 | bytes 4732932 | tf_op jit(solution)/shard_map/while/body/eval_jaxpr/dot_general | solution.py:62
  132.6 2.4 %fusion.28 = f32[512,1024]{1,0:T(8,128)S(1)} fusion(bf16[512,2048]{1,0:T(8,128)(2,1)S(1)} %get-tuple-element.106, bf16[2048,1024]{1,0:T(8,128)(2,1)S(1)} %copy-done.2), kind=kOutput, calls=%fused_computation.24.clone.1 | convolution fusion | flops 2147483648 | bytes 8388608 | tf_op jit(solution)/shard_map/while/body/eval_jaxpr/dot_general | solution.py:67
  135.0 1.1 fusion.29
  136.3 3.3 %convert_reduce_fusion.3 = (f32[512]{0:T(512)S(1)}, bf16[512,2048]{1,0:T(8,128)(2,1)S(1)}) fusion(bf16[2048,512]{1,0:T(8,128)(2,1)} %get-tuple-element.129, f32[512]{0:T(512)S(1)} %get-tuple-element.127, bf16[4,512,512]{2,1,0:T(8,128)(2,1)S(1)} %get-tuple-element.126, s32[]{:T(128)} %get-tuple-element.116, f32[2048]{0:T(1024)S(1)} %get-tuple-element.128, ...), kind=kOutput, calls=%fused_computation.clone.1 | convolution fusion | flops 1081867776 | bytes 4732932 | tf_op jit(solution)/shard_map/while/body/eval_jaxpr/dot_general | solution.py:62
  139.6 2.4 %fusion.28 = f32[512,1024]{1,0:T(8,128)S(1)} fusion(bf16[512,2048]{1,0:T(8,128)(2,1)S(1)} %get-tuple-element.106, bf16[2048,1024]{1,0:T(8,128)(2,1)S(1)} %copy-done.2), kind=kOutput, calls=%fused_computation.24.clone.1 | convolution fusion | flops 2147483648 | bytes 8388608 | tf_op jit(solution)/shard_map/while/body/eval_jaxpr/dot_general | solution.py:67
  142.0 1.1 fusion.29
  143.3 3.3 %convert_reduce_fusion.3 = (f32[512]{0:T(512)S(1)}, bf16[512,2048]{1,0:T(8,128)(2,1)S(1)}) fusion(bf16[2048,512]{1,0:T(8,128)(2,1)} %get-tuple-element.129, f32[512]{0:T(512)S(1)} %get-tuple-element.127, bf16[4,512,512]{2,1,0:T(8,128)(2,1)S(1)} %get-tuple-element.126, s32[]{:T(128)} %get-tuple-element.116, f32[2048]{0:T(1024)S(1)} %get-tuple-element.128, ...), kind=kOutput, calls=%fused_computation.clone.1 | convolution fusion | flops 1081867776 | bytes 4732932 | tf_op jit(solution)/shard_map/while/body/eval_jaxpr/dot_general | solution.py:62
  146.5 2.4 %fusion.28 = f32[512,1024]{1,0:T(8,128)S(1)} fusion(bf16[512,2048]{1,0:T(8,128)(2,1)S(1)} %get-tuple-element.106, bf16[2048,1024]{1,0:T(8,128)(2,1)S(1)} %copy-done.2), kind=kOutput, calls=%fused_computation.24.clone.1 | convolution fusion | flops 2147483648 | bytes 8388608 | tf_op jit(solution)/shard_map/while/body/eval_jaxpr/dot_general | solution.py:67
  150.2 3.3 %convert_reduce_fusion.3 = (f32[512]{0:T(512)S(1)}, bf16[512,2048]{1,0:T(8,128)(2,1)S(1)}) fusion(bf16[2048,512]{1,0:T(8,128)(2,1)} %get-tuple-element.129, f32[512]{0:T(512)S(1)} %get-tuple-element.127, bf16[4,512,512]{2,1,0:T(8,128)(2,1)S(1)} %get-tuple-element.126, s32[]{:T(128)} %get-tuple-element.116, f32[2048]{0:T(1024)S(1)} %get-tuple-element.128, ...), kind=kOutput, calls=%fused_computation.clone.1 | convolution fusion | flops 1081867776 | bytes 4732932 | tf_op jit(solution)/shard_map/while/body/eval_jaxpr/dot_general | solution.py:62
  153.5 2.4 %fusion.28 = f32[512,1024]{1,0:T(8,128)S(1)} fusion(bf16[512,2048]{1,0:T(8,128)(2,1)S(1)} %get-tuple-element.106, bf16[2048,1024]{1,0:T(8,128)(2,1)S(1)} %copy-done.2), kind=kOutput, calls=%fused_computation.24.clone.1 | convolution fusion | flops 2147483648 | bytes 8388608 | tf_op jit(solution)/shard_map/while/body/eval_jaxpr/dot_general | solution.py:67
  155.9 1.1 fusion.29
  156.9 1.8 copy.7
  158.7 6.6 %all_to_all.21 = bf16[2,8,128,512]{3,2,1,0:T(8,128)(2,1)S(1)} all-to-all(bf16[2,8,128,512]{3,2,1,0:T(8,128)(2,1)S(1)} %copy.7), channel_id=1, replica_groups=mesh['gx_0'=2,'gx_1'=4,'gx_2'=2,'gy'=8,'gz'=2] {'gx_2'}, dimensions={0} | all-to-all | bytes 4194304 | tf_op jit(solution)/shard_map/all_to_all | solution.py:44
  166.4 21.6 %all_to_all.22 = bf16[8,128,512]{2,1,0:T(8,128)(2,1)S(1)} all-to-all(bf16[8,128,512]{2,1,0:T(8,128)(2,1)S(1)} %reduce_sum.49), channel_id=1, replica_groups=mesh['gx_0'=2,'gx_1'=4,'gx_2'=2,'gy'=8,'gz'=2] {'gx_0','gx_1'}, dimensions={0} | all-to-all | bytes 2097152 | tf_op jit(solution)/shard_map/all_to_all | solution.py:52
  (32 shorter events, 6.2 us)
Async XLA Ops:
  6.5 115.0 %all-gather.2.cloned.1.call-start = ((), (), s32[]{:S(2)}) async-start(), calls=%async_computation.4 | async-start | bytes 4456448 | tf_op jit(solution)/shard_map/all_gather | solution.py:32
  7.5 10.3 %copy-start.3 = (s32[512]{0:T(512)S(1)}, s32[512]{0:T(512)}, u32[]{:S(2)}) copy-start(s32[512]{0:T(512)} %param.7) | copy-start | bytes 6148
  10.3 25.6 %all-to-all-start = ((bf16[8,128,512]{2,1,0:T(8,128)(2,1)}), bf16[8,128,512]{2,1,0:T(8,128)(2,1)S(1)}, u32[]{:S(2)}, u32[]{:S(2)}) async-start(bf16[8,128,512]{2,1,0:T(8,128)(2,1)} %broadcast_in_dim.10), calls=%async_computation | async-start | bytes 2097152 | tf_op jit(solution)/shard_map/all_to_all | solution.py:13
  124.0 3.2 %copy-start.1 = (bf16[2048,512]{1,0:T(8,128)(2,1)}, bf16[2048,512]{1,0:T(8,128)(2,1)S(1)}, u32[]{:S(2)}) copy-start(bf16[2048,512]{1,0:T(8,128)(2,1)S(1)} %get-tuple-element.113) | copy-start | bytes 6291460
  124.0 4.5 %copy-start = (bf16[2048,1024]{1,0:T(8,128)(2,1)S(1)}, bf16[2048,1024]{1,0:T(8,128)(2,1)}, u32[]{:S(2)}) copy-start(bf16[2048,1024]{1,0:T(8,128)(2,1)} %all-gather.2.cloned.1.call-done) | copy-start | bytes 12582916
  129.3 3.3 %copy-start.2 = (bf16[2048,1024]{1,0:T(8,128)(2,1)S(1)}, bf16[2048,1024]{1,0:T(8,128)(2,1)}, u32[]{:S(2)}) copy-start(bf16[2048,1024]{1,0:T(8,128)(2,1)} %get-tuple-element.130) | copy-start | bytes 12582916 | tf_op jit(solution)/shard_map/while
  136.3 3.3 %copy-start.2 = (bf16[2048,1024]{1,0:T(8,128)(2,1)S(1)}, bf16[2048,1024]{1,0:T(8,128)(2,1)}, u32[]{:S(2)}) copy-start(bf16[2048,1024]{1,0:T(8,128)(2,1)} %get-tuple-element.130) | copy-start | bytes 12582916 | tf_op jit(solution)/shard_map/while
  143.3 3.3 %copy-start.2 = (bf16[2048,1024]{1,0:T(8,128)(2,1)S(1)}, bf16[2048,1024]{1,0:T(8,128)(2,1)}, u32[]{:S(2)}) copy-start(bf16[2048,1024]{1,0:T(8,128)(2,1)} %get-tuple-element.130) | copy-start | bytes 12582916 | tf_op jit(solution)/shard_map/while
  150.2 3.3 %copy-start.2 = (bf16[2048,1024]{1,0:T(8,128)(2,1)S(1)}, bf16[2048,1024]{1,0:T(8,128)(2,1)}, u32[]{:S(2)}) copy-start(bf16[2048,1024]{1,0:T(8,128)(2,1)} %get-tuple-element.130) | copy-start | bytes 12582916 | tf_op jit(solution)/shard_map/while
Sparse Core Ops, SparseCore 0:
  9.3 112.1 all-gather.1
where the time goes:
time: 196 us
  waiting for transfers between devices  97.2 us (50%)
  blocking collectives  34.4 us (18%)
  matrix products  22.5 us (11%)
  between operations  13.5 us (7%)
  other arithmetic  13 us (7%)
  local copies, waits for them, and re-layouts  7.54 us (4%)
  starting transfers between devices  7.47 us (4%)
    all_gather x1, waiting for transfers between devices, side_by_side(): result = lax.all_gather(both, axis, axis=dim, tiled=True)  79.1 us
    all_to_all x1, blocking collectives, sum_by_axis(): lax.all_to_all(nearer.astype(jnp.bfloat16), far, split_axis=0, concat_axi...  21.6 us
    all_to_all x1, waiting for transfers between devices, sent_to_all(): return lax.all_to_all(copies, axis, split_axis=0, concat_axis=0, tiled=True)  18.1 us
    dot_general x4, matrix products, kernel_terms(): lax.dot_general(scaled, sources, (((1,), (1,)), ((), ())), preferred_elem...  13.1 us
    dot_general x4, matrix products, kernel_terms(): products = jnp.dot(kernel, stacked, preferred_element_type=jnp.float32)  9.47 us
    all_to_all x1, starting transfers between devices, sent_to_all(): return lax.all_to_all(copies, axis, split_axis=0, concat_axis=0, tiled=True)  7.47 us
    all_to_all x1, blocking collectives, summed_on_arrival(): lax.all_to_all(tiles, axis, split_axis=0, concat_axis=0, tiled=True)  6.64 us
    all_to_all x1, blocking collectives, sent_to_all(): return lax.all_to_all(copies, axis, split_axis=0, concat_axis=0, tiled=True)  6.13 us
  transfers between devices with their start and end apart: 2, of which 2 were waited for; matrix products, arithmetic and copies ran while one was open for 1% of the time, Pallas kernels for 0%

commit v1 on v0

v1 whole, which is shorter than its diff:
```python
import functools

import jax
import jax.numpy as jnp
from jax import lax
from jax.experimental import pallas as pl
from jax.experimental.pallas import tpu as pltpu
from jax.sharding import PartitionSpec as P

F32 = jnp.float32
BF16 = jnp.bfloat16
LOG2E = 1.4426950408889634
ROWS = 128
D = 512
GROUPS = 1
W = D // GROUPS
HALF = ROWS // 2
QUARTER = ROWS // 4
TILE = 4 * HALF
COPIES = 400


def neighbours():
    gx, gy, gz = lax.axis_index("gx"), lax.axis_index("gy"), lax.axis_index("gz")
    y_hi, x, core = gx // 8, (gx // 2) % 4, gx % 2
    y = y_hi * 2 + gz

    def at(x, y, z, core):
        return {"gx": (y // 2) * 8 + x * 2 + core, "gy": z, "gz": y % 2}

    ids = {"core": at(x, y, gy, 1 - core)}
    for step in (1, -1):
        ids["x", step] = at((x + step + 4) % 4, y, gy, core)
        ids["y", step] = at(x, (y + step + 4) % 4, gy, core)
        ids["z", step] = at(x, y, (gy + step + 8) % 8, core)
    return ids


def kernel(
    particles_hbm, scores_hbm, power_ref, out_ref,
    particles, scores, targets, sources, source_scores, kernels, acc,
    target_squares, source_squares, totals, inverse,
    sent, relay, arrived, sent2, relay2, arrived2,
    load_sem, send_sem, recv_sem,
):
    loads = [
        pltpu.make_async_copy(particles_hbm, particles, load_sem.at[0]),
        pltpu.make_async_copy(scores_hbm, scores, load_sem.at[1]),
    ]
    for load in loads:
        load.start()
    ids = neighbours()
    barrier = pltpu.get_barrier_semaphore()
    for device in ids.values():
        pl.semaphore_signal(barrier, inc=1, device_id=device, device_id_type=pl.DeviceIdType.MESH)

    copies = {}

    def copy(name, src, dst, device):
        n = len(copies)
        made = pltpu.make_async_remote_copy(
            src_ref=src, dst_ref=dst, send_sem=send_sem.at[n], recv_sem=recv_sem.at[n],
            device_id=ids[device], device_id_type=pl.DeviceIdType.MESH,
        )
        assert name not in copies
        copies[name] = made
        made.start()

    def arrive(name):
        copies[name].wait_recv()

    weights = jnp.exp2(-power_ref[...].astype(F32))
    for load in loads:
        load.wait()
    rounded = particles[...].astype(BF16)
    rounded_f = rounded.astype(F32)
    double = rounded_f * (2.0 * weights)
    targets[0, 0, 0:HALF] = rounded[:HALF]
    targets[1, 0, 0:HALF] = rounded[HALF:]
    sources[0, 0] = double.T.astype(BF16)
    folded = (scores[...].astype(F32) - double).astype(BF16)
    for g in range(GROUPS):
        source_scores[g, 0, 0:ROWS] = folded[:, g * W : (g + 1) * W]
    inverse[...] = jnp.broadcast_to(0.25 / weights, (ROWS, D)).T

    pl.semaphore_wait(barrier, len(ids))

    def slot(step, h):
        return h if step == 1 else 8 - h

    def z_rows(h_next, step, size):
        if h_next < 4:
            return pl.ds(0, size)
        return pl.ds(0, size // 2) if step == 1 else pl.ds(size // 2, size // 2)

    def z_send(kind, h):
        for step in (1, -1):
            src, dst = slot(step, h) % 8, slot(step, h + 1)
            if kind == "r":
                rows = z_rows(h + 1, step, D)
                a, b = sources.at[src, 0, rows], sources.at[dst, 0, rows]
            else:
                rows = z_rows(h + 1, step, ROWS)
                a, b = source_scores.at[kind, src, rows], source_scores.at[kind, dst, rows]
            copy(("z", kind, h + 1, step), a, b, ("z", step))

    def z_arrive(kind, h):
        for step in (1, -1):
            arrive(("z", kind, h, step))

    def to_core(kind, s):
        if kind == "r":
            copy(("core", kind, s), sources.at[s, 0], sources.at[s, 1], "core")
        else:
            copy(
                ("core", kind, s),
                source_scores.at[kind, s, pl.ds(0, ROWS)],
                source_scores.at[kind, s, pl.ds(ROWS, ROWS)],
                "core",
            )

    def z_step(kind, h):
        z_arrive(kind, h)
        if h < 4:
            z_send(kind, h)
        for s in {h, 8 - h}:
            to_core(kind, s)

    axes = (("x", "y"), ("y", "x"))

    def t_first(half):
        for step, land in ((1, 3), (-1, 1)):
            copy(
                ("c1", half, step),
                targets.at[half, 0, pl.ds(0, HALF)],
                targets.at[half, 0, pl.ds(land * HALF, HALF)],
                (axes[half][0], step),
            )

    def t_first_relay(half):
        for step, src, part in ((1, 3, 0), (-1, 1, QUARTER)):
            copy(
                ("c2", half, step),
                targets.at[half, 0, pl.ds(src * HALF + part, QUARTER)],
                targets.at[half, 0, pl.ds(2 * HALF + part, QUARTER)],
                (axes[half][0], step),
            )

    def t_second(half, i):
        for step, land in ((1, 3), (-1, 1)):
            copy(
                ("c3", half, i, step),
                targets.at[half, 0, pl.ds(i * HALF, HALF)],
                targets.at[half, land, pl.ds(i * HALF, HALF)],
                (axes[half][1], step),
            )

    def t_second_relay(half, i):
        for step, src, part in ((1, 3, 0), (-1, 1, QUARTER)):
            copy(
                ("c6", half, i, step),
                targets.at[half, src, pl.ds(i * HALF + part, QUARTER)],
                targets.at[half, 2, pl.ds(i * HALF + part, QUARTER)],
                (axes[half][1], step),
            )

    def t_arrive(name, *at):
        for half in (0, 1):
            for step in (1, -1):
                arrive((name, half, *at, step))

    def square_targets(half, s):
        rows = targets[half, s].astype(F32)
        total = jnp.sum(rows * rows * weights, axis=1, keepdims=True) * LOG2E
        target_squares[half, s] = jnp.broadcast_to(total, (TILE, 128))

    def square_sources(s):
        for core in (0, 1):
            part = sources[s, core].astype(F32)
            total = jnp.sum(part * part * inverse[...], axis=0, keepdims=True) * LOG2E
            source_squares[s, :, core * 128 : core * 128 + 128] = total

    def make_kernels(tiles, slots):
        for half, s in tiles:
            for k in slots:
                both = jnp.concatenate([sources[k, 0], sources[k, 1]], axis=1)
                inner = jnp.dot(targets[half, s], both, preferred_element_type=F32)
                own = target_squares[half, s]
                power = inner * LOG2E - jnp.concatenate([own, own], axis=1) - source_squares[k]
                values = jnp.exp2(power).astype(BF16)
                kernels[half, s, k] = values
                values = values.astype(F32)
                pair = values[:, :128] + values[:, 128:]
                if k == 0:
                    totals[half, s] = pair
                else:
                    totals[half, s] += pair

    def product(g, half, s, slots):
        left = jnp.concatenate([kernels[half, s, k] for k in slots], axis=1)
        right = jnp.concatenate([source_scores[g, k] for k in slots], axis=0)
        return jnp.dot(left, right, preferred_element_type=F32)

    def add_products(g, tiles, slots):
        for half, s in tiles:
            if 0 in slots:
                acc[g, half, s] = product(g, half, s, slots)
            else:
                acc[g, half, s] += product(g, half, s, slots)

    def last_product(g, half, s, slots):
        row_totals = jnp.sum(totals[half, s], axis=1, keepdims=True)
        rows = targets[half, s].astype(F32)[:, g * W : (g + 1) * W]
        scale = 2.0 * weights[:, g * W : (g + 1) * W]
        result = acc[g, half, s] + product(g, half, s, slots) + rows * scale * row_totals
        acc[g, half, s] = result
        sent[g, half, s, 0:HALF] = result[2 * HALF : 3 * HALF].astype(BF16)
        sent[g, half, s, HALF : HALF + QUARTER] = result[HALF + QUARTER : 2 * HALF].astype(BF16)
        sent[g, half, s, HALF + QUARTER : TILE // 2] = result[3 * HALF : 3 * HALF + QUARTER].astype(BF16)

    def q4(n):
        return pl.ds(n * QUARTER, QUARTER)

    def first_send(g, half, s):
        axis = axes[half][0]
        base = sent.at[g, half, s]
        copy(("rel", g, half, s, 1), base.at[q4(0)], relay.at[g, half, s, q4(0)], (axis, 1))
        copy(("rel", g, half, s, -1), base.at[q4(1)], relay.at[g, half, s, q4(1)], (axis, -1))

    def first_send_plain(g, half, s):
        axis = axes[half][0]
        base = sent.at[g, half, s]
        copy(("pln", g, half, s, 1), base.at[q4(2)], arrived.at[g, half, s, q4(1)], (axis, 1))
        copy(("pln", g, half, s, -1), base.at[q4(3)], arrived.at[g, half, s, q4(2)], (axis, -1))

    def first_add(g, half, s):
        for step in (1, -1):
            arrive(("rel", g, half, s, step))
        summed = acc[g, half, s, pl.ds(HALF, QUARTER)] + relay[g, half, s, q4(0)].astype(F32)
        sent[g, half, s, q4(4)] = summed.astype(BF16)
        summed = acc[g, half, s, pl.ds(3 * HALF + QUARTER, QUARTER)] + relay[g, half, s, q4(1)].astype(F32)
        sent[g, half, s, q4(5)] = summed.astype(BF16)

    def first_send_added(g, half, s):
        axis = axes[half][0]
        base = sent.at[g, half, s]
        copy(("add", g, half, s, 1), base.at[q4(4)], arrived.at[g, half, s, q4(0)], (axis, 1))
        copy(("add", g, half, s, -1), base.at[q4(5)], arrived.at[g, half, s, q4(3)], (axis, -1))

    def first_result(g, half, s):
        for name in ("pln", "add"):
            for step in (1, -1):
                arrive((name, g, half, s, step))
        own = acc[g, half, s, pl.ds(0, HALF)]
        came = arrived[g, half, s].astype(F32)
        return own + came[:HALF] + came[HALF:]

    def second_prepare(g, half, s):
        result = first_result(g, half, s)
        if s == 2:
            sent2[g, half, pl.ds(0, HALF)] = result.astype(BF16)
        elif s == 1:
            sent2[g, half, q4(2)] = result[QUARTER:].astype(BF16)
            acc[g, half, 1, pl.ds(0, QUARTER)] = result[:QUARTER]
        elif s == 3:
            sent2[g, half, q4(3)] = result[:QUARTER].astype(BF16)
            acc[g, half, 3, pl.ds(0, QUARTER)] = result[QUARTER:]
        else:
            acc[g, half, 0, pl.ds(0, HALF)] = result

    def second_send(g, half, s):
        axis = axes[half][1]
        base = sent2.at[g, half]
        if s == 2:
            copy(("rel2", g, half, 1), base.at[q4(0)], relay2.at[g, half, q4(0)], (axis, 1))
            copy(("rel2", g, half, -1), base.at[q4(1)], relay2.at[g, half, q4(1)], (axis, -1))
        elif s == 1:
            copy(("pln2", g, half, 1), base.at[q4(2)], arrived2.at[g, half, q4(1)], (axis, 1))
        elif s == 3:
            copy(("pln2", g, half, -1), base.at[q4(3)], arrived2.at[g, half, q4(2)], (axis, -1))

    def second_add(g, half):
        for step in (1, -1):
            arrive(("rel2", g, half, step))
        summed = acc[g, half, 1, pl.ds(0, QUARTER)] + relay2[g, half, q4(0)].astype(F32)
        sent2[g, half, q4(4)] = summed.astype(BF16)
        summed = acc[g, half, 3, pl.ds(0, QUARTER)] + relay2[g, half, q4(1)].astype(F32)
        sent2[g, half, q4(5)] = summed.astype(BF16)

    def second_send_added(g, half):
        axis = axes[half][1]
        base = sent2.at[g, half]
        copy(("add2", g, half, 1), base.at[q4(4)], arrived2.at[g, half, q4(0)], (axis, 1))
        copy(("add2", g, half, -1), base.at[q4(5)], arrived2.at[g, half, q4(3)], (axis, -1))

    def second_result(g, half):
        for name in ("pln2", "add2"):
            for step in (1, -1):
                arrive((name, g, half, step))
        came = arrived2[g, half].astype(F32)
        result = acc[g, half, 0, pl.ds(0, HALF)] + came[:HALF] + came[HALF:]
        out_ref[half * HALF : half * HALF + HALF, g * W : (g + 1) * W] = result

    groups = tuple(range(GROUPS))
    near = [(0, 0), (1, 0)]
    middle = [(half, s) for s in (1, 3) for half in (0, 1)]
    far = [(0, 2), (1, 2)]
    every = near + middle + far

    z_send("r", 0)
    to_core("r", 0)
    for half in (0, 1):
        t_first(half)
    for half in (0, 1):
        t_second(half, 0)
    for g in groups:
        z_send(g, 0)
        to_core(g, 0)

    t_arrive("c1")
    for half in (0, 1):
        t_first_relay(half)
    for i in (3, 1):
        for half in (0, 1):
            t_second(half, i)
    t_arrive("c3", 0)
    for half in (0, 1):
        t_second_relay(half, 0)
    arrive(("core", "r", 0))
    square_sources(0)
    z_step("r", 1)
    t_arrive("c2")
    for half in (0, 1):
        t_second(half, 2)
    for tile in near:
        square_targets(*tile)
    make_kernels(near, (0,))
    for g in groups:
        z_step(g, 1)
    for i in (3, 1):
        t_arrive("c3", i)
        for half in (0, 1):
            t_second_relay(half, i)
    t_arrive("c3", 2)
    for half in (0, 1):
        t_second_relay(half, 2)
    for s in (1, 7):
        arrive(("core", "r", s))
        square_sources(s)
    for tile in middle:
        square_targets(*tile)
    make_kernels(middle, (0,))
    make_kernels(near, (1, 7))
    z_step("r", 2)
    make_kernels(middle, (1, 7))
    for g in groups:
        z_step(g, 2)
    for i in range(4):
        t_arrive("c6", i)
    for tile in far:
        square_targets(*tile)
    make_kernels(far, (0, 1, 7))
    for g in groups:
        for s in (0, 1, 7):
            arrive(("core", g, s))
        add_products(g, every, (0, 1, 7))
    for s in (2, 6):
        arrive(("core", "r", s))
        square_sources(s)
    make_kernels(every, (2, 6))
    z_step("r", 3)
    for g in groups:
        for s in (2, 6):
            arrive(("core", g, s))
        add_products(g, every, (2, 6))
    for s in (3, 5):
        arrive(("core", "r", s))
        square_sources(s)
    make_kernels(every, (3, 5))
    for g in groups:
        z_step(g, 3)
    z_step("r", 4)
    for g in groups:
        for s in (3, 5):
            arrive(("core", g, s))
        add_products(g, every, (3, 5))
    arrive(("core", "r", 4))
    square_sources(4)
    make_kernels(every, (4,))
    for g in groups:
        z_step(g, 4)

    order = [(half, s) for s in (2, 1, 3, 0) for half in (0, 1)]
    for g in groups:
        arrive(("core", g, 4))
        before = None
        for tile in order + [None]:
            if tile is not None:
                last_product(g, *tile, (4,))
            if before is not None:
                first_send(g, *before)
                first_send_plain(g, *before)
            before = tile
        before = None
        for tile in order + [None]:
            if tile is not None:
                first_add(g, *tile)
            if before is not None:
                first_send_added(g, *before)
            before = tile
        before = None
        for tile in order + [None]:
            if tile is not None:
                second_prepare(g, *tile)
            if before is not None:
                second_send(g, *before)
            before = tile
        for half in (0, 1):
            second_add(g, half)
        for half in (0, 1):
            second_send_added(g, half)
        for half in (0, 1):
            second_result(g, half)

    for made in copies.values():
        made.wait_send()
    assert len(copies) <= COPIES


def local(particles, scores, power):
    return pl.pallas_call(
        kernel,
        out_shape=jax.ShapeDtypeStruct((ROWS, D), F32),
        in_specs=[
            pl.BlockSpec(memory_space=pl.ANY),
            pl.BlockSpec(memory_space=pl.ANY),
            pl.BlockSpec(memory_space=pltpu.VMEM),
        ],
        out_specs=pl.BlockSpec(memory_space=pltpu.VMEM),
        scratch_shapes=[
            pltpu.VMEM((ROWS, D), F32),
            pltpu.VMEM((ROWS, D), BF16),
            pltpu.VMEM((2, 4, TILE, D), BF16),
            pltpu.VMEM((8, 2, D, ROWS), BF16),
            pltpu.VMEM((GROUPS, 8, 2 * ROWS, W), BF16),
            pltpu.VMEM((2, 4, 8, TILE, 2 * ROWS), BF16),
            pltpu.VMEM((GROUPS, 2, 4, TILE, W), F32),
            pltpu.VMEM((2, 4, TILE, 128), F32),
            pltpu.VMEM((8, 1, 2 * ROWS), F32),
            pltpu.VMEM((2, 4, TILE, 128), F32),
            pltpu.VMEM((D, ROWS), F32),
            pltpu.VMEM((GROUPS, 2, 4, 6 * QUARTER, W), BF16),
            pltpu.VMEM((GROUPS, 2, 4, 2 * QUARTER, W), BF16),
            pltpu.VMEM((GROUPS, 2, 4, 4 * QUARTER, W), BF16),
            pltpu.VMEM((GROUPS, 2, 6 * QUARTER, W), BF16),
            pltpu.VMEM((GROUPS, 2, 2 * QUARTER, W), BF16),
            pltpu.VMEM((GROUPS, 2, 4 * QUARTER, W), BF16),
            pltpu.SemaphoreType.DMA((2,)),
            pltpu.SemaphoreType.DMA((COPIES,)),
            pltpu.SemaphoreType.DMA((COPIES,)),
        ],
        compiler_params=pltpu.CompilerParams(
            collective_id=0, has_side_effects=True, vmem_limit_bytes=56 * 2**20
        ),
    )(particles, scores, power.reshape(1, D))


def solution(mesh):
    split = P(("gx", "gy", "gz"), None)
    return jax.shard_map(
        local, mesh=mesh, in_specs=(split, split, P()), out_specs=split, check_vma=False
    )
```

time: 196 us -> 63.3 us (0.32)
  waiting for transfers between devices: 97.2 us -> 0 us
  Pallas kernels: 0 us -> 61.5 us
  blocking collectives: 34.4 us -> 0 us
  matrix products: 22.5 us -> 0 us
  between operations: 13.5 us -> 0.01 us
  other arithmetic: 13 us -> 0 us
  starting transfers between devices: 7.47 us -> 0 us
  local copies, waits for them, and re-layouts: 7.54 us -> 1.67 us
    all_gather x1 -> x0, waiting for transfers between devices: 79.1 us -> none  [side_by_side(): result = lax.all_gather(both, axis, axis=dim, tiled=True)]
    pallas_call x0 -> x1, Pallas kernels: none -> 61.5 us  [local(): pl.pallas_call(kernel, out_shape=jax.ShapeDtypeStruct((ROWS, D), F32), in...]
    all_to_all x3 -> x0, blocking collectives: 34.4 us -> none  [the longest x1 21.6 us: sum_by_axis(): lax.all_to_all(nearer.astype(jnp.bfloat16), far, split_axis=0, concat_axi...]
    dot_general x8 -> x0, matrix products: 22.5 us -> none  [the longest x4 13.1 us: kernel_terms(): lax.dot_general(scaled, sources, (((1,), (1,)), ((), ())), preferred_elem...]
    all_to_all x1 -> x0, waiting for transfers between devices: 18.1 us -> none  [sent_to_all(): return lax.all_to_all(copies, axis, split_axis=0, concat_axis=0, tiled=True)]
    all_to_all x1 -> x0, starting transfers between devices: 7.47 us -> none  [sent_to_all(): return lax.all_to_all(copies, axis, split_axis=0, concat_axis=0, tiled=True)]
    concatenate x2 -> x0, other arithmetic: 4.41 us -> none  [the longest x1 2.78 us: make_terms(): stacked = jnp.concatenate([source_scores, sources], axis=1)]
    dynamic_update_slice x4 -> x0, other arithmetic: 4.33 us -> none  [term_rows(): return lax.map(one_block, target_blocks).reshape(count, width)]
  transfers between devices with their start and end apart: 2 -> 0, of which waited for: 2 -> 0; matrix products, arithmetic and copies ran while one was open for 1% -> 0% of each run, Pallas kernels for 0% -> 0%
where the time goes in v1:
time: 63.3 us; the launch traced here: 63.2 us
  Pallas kernels  61.5 us (97%)
  local copies, waits for them, and re-layouts  1.67 us (3%)
    pallas_call x1, Pallas kernels, local(): pl.pallas_call(kernel, out_shape=jax.ShapeDtypeStruct((ROWS, D), F32), in...  61.5 us
    unnamed x1, local copies, waits for them, and re-layouts  1.67 us

profile of v1, /device:TPU:1, one launch (start us, length us, event | category | flops | bytes accessed | tf_op | source)
XLA Modules:
  0.0 63.2 jit_solution(426308414578561355)
XLA Ops:
  0.0 61.5 %shard_map.37 = f32[128,512]{1,0:T(8,128)} custom-call(f32[128,512]{1,0:T(8,128)} %particles_hbm.1, bf16[128,512]{1,0:T(8,128)(2,1)} %scores_hbm.1, s32[1,512]{1,0:T(1,128)} %bitcast.1), custom_call_target="tpu_custom_call" | custom-call | tf_op jit(solution)/shard_map/pallas_call | solution.py:431
  61.5 1.7 %copy.5 = f32[128,512]{1,0:T(8,128)} copy(f32[128,512]{1,0:T(8,128)} %shard_map.37) | data formatting | bytes 524288

commit v2 on v1

--- a/solution.py
+++ b/solution.py
@@ -17,7 +17,7 @@
 HALF = ROWS // 2
 QUARTER = ROWS // 4
 TILE = 4 * HALF
-COPIES = 400
+COPIES = 172
 
 
 def neighbours():
@@ -34,6 +34,15 @@
         ids["y", step] = at(x, (y + step + 4) % 4, gy, core)
         ids["z", step] = at(x, y, (gy + step + 8) % 8, core)
     return ids
+
+
+def scoped_kernel(*refs):
+    pl.run_scoped(
+        functools.partial(kernel, *refs),
+        pltpu.SemaphoreType.DMA((2,)),
+        pltpu.SemaphoreType.DMA((COPIES,)),
+        pltpu.SemaphoreType.DMA((COPIES,)),
+    )
 
 
 def kernel(
@@ -88,25 +97,20 @@
     def slot(step, h):
         return h if step == 1 else 8 - h
 
-    def z_rows(h_next, step, size):
-        if h_next < 4:
-            return pl.ds(0, size)
-        return pl.ds(0, size // 2) if step == 1 else pl.ds(size // 2, size // 2)
-
-    def z_send(kind, h):
+    def piece(size, step, n):
+        first = 0 if step == 1 else 1
+        return pl.ds((first + n) % 2 * (size // 2), size // 2)
+
+    def z_send(kind, h, n):
         for step in (1, -1):
             src, dst = slot(step, h) % 8, slot(step, h + 1)
             if kind == "r":
-                rows = z_rows(h + 1, step, D)
+                rows = piece(D, step, n)
                 a, b = sources.at[src, 0, rows], sources.at[dst, 0, rows]
             else:
-                rows = z_rows(h + 1, step, ROWS)
+                rows = piece(ROWS, step, n)
                 a, b = source_scores.at[kind, src, rows], source_scores.at[kind, dst, rows]
-            copy(("z", kind, h + 1, step), a, b, ("z", step))
-
-    def z_arrive(kind, h):
-        for step in (1, -1):
-            arrive(("z", kind, h, step))
+            copy(("z", kind, h + 1, n, step), a, b, ("z", step))
 
     def to_core(kind, s):
         if kind == "r":
@@ -119,12 +123,14 @@
                 "core",
             )
 
-    def z_step(kind, h):
-        z_arrive(kind, h)
-        if h < 4:
-            z_send(kind, h)
-        for s in {h, 8 - h}:
-            to_core(kind, s)
+    def z_step(kind, h, n):
+        for step in (1, -1):
+            arrive(("z", kind, h, n, step))
+        if h < 3 or (h == 3 and n == 0):
+            z_send(kind, h, n)
+        if n == 1 or h == 4:
+            for s in sorted({h, 8 - h}):
+                to_core(kind, s)
 
     axes = (("x", "y"), ("y", "x"))
 
@@ -301,126 +307,134 @@
         result = acc[g, half, 0, pl.ds(0, HALF)] + came[:HALF] + came[HALF:]
         out_ref[half * HALF : half * HALF + HALF, g * W : (g + 1) * W] = result
 
-    groups = tuple(range(GROUPS))
     near = [(0, 0), (1, 0)]
     middle = [(half, s) for s in (1, 3) for half in (0, 1)]
     far = [(0, 2), (1, 2)]
     every = near + middle + far
-
-    z_send("r", 0)
-    to_core("r", 0)
-    for half in (0, 1):
-        t_first(half)
-    for half in (0, 1):
-        t_second(half, 0)
-    for g in groups:
-        z_send(g, 0)
-        to_core(g, 0)
-
-    t_arrive("c1")
-    for half in (0, 1):
-        t_first_relay(half)
-    for i in (3, 1):
-        for half in (0, 1):
-            t_second(half, i)
-    t_arrive("c3", 0)
-    for half in (0, 1):
-        t_second_relay(half, 0)
-    arrive(("core", "r", 0))
+    both = (0, 1)
+
+    def from_core(kind, slots):
+        for s in slots:
+            arrive(("core", kind, s))
+
+    def start():
+        z_send("r", 0, 0)
+        for half in both:
+            t_first(half)
+        for half in both:
+            t_second(half, 0)
+        z_send("r", 0, 1)
+        to_core("r", 0)
+        z_send(0, 0, 0)
+        z_send(0, 0, 1)
+        to_core(0, 0)
+
+    def t_step1():
+        t_arrive("c1")
+        for half in both:
+            t_first_relay(half)
+        for i in (3, 1):
+            for half in both:
+                t_second(half, i)
+
+    def t_step2():
+        t_arrive("c2")
+        for half in both:
+            t_second(half, 2)
+        t_arrive("c3", 0)
+        for half in both:
+            t_second_relay(half, 0)
+
+    def t_step3(i):
+        t_arrive("c3", i)
+        for half in both:
+            t_second_relay(half, i)
+
+    def t_step4():
+        for i in range(4):
+            t_arrive("c6", i)
+
+    start()
+    t_step1()
+    z_step("r", 1, 0)
+    z_step("r", 1, 1)
+    from_core("r", (0,))
     square_sources(0)
-    z_step("r", 1)
-    t_arrive("c2")
-    for half in (0, 1):
-        t_second(half, 2)
+    z_step(0, 1, 0)
+    t_step2()
     for tile in near:
         square_targets(*tile)
     make_kernels(near, (0,))
-    for g in groups:
-        z_step(g, 1)
-    for i in (3, 1):
-        t_arrive("c3", i)
-        for half in (0, 1):
-            t_second_relay(half, i)
-    t_arrive("c3", 2)
-    for half in (0, 1):
-        t_second_relay(half, 2)
-    for s in (1, 7):
-        arrive(("core", "r", s))
-        square_sources(s)
+    z_step(0, 1, 1)
+    t_step3(3)
+    from_core("r", (1, 7))
+    square_sources(1)
+    square_sources(7)
+    z_step("r", 2, 0)
+    t_step3(1)
+    make_kernels(near, (1, 7))
+    z_step("r", 2, 1)
+    t_step3(2)
     for tile in middle:
         square_targets(*tile)
     make_kernels(middle, (0,))
-    make_kernels(near, (1, 7))
-    z_step("r", 2)
+    z_step(0, 2, 0)
     make_kernels(middle, (1, 7))
-    for g in groups:
-        z_step(g, 2)
-    for i in range(4):
-        t_arrive("c6", i)
+    z_step(0, 2, 1)
+    t_step4()
     for tile in far:
         square_targets(*tile)
     make_kernels(far, (0, 1, 7))
-    for g in groups:
-        for s in (0, 1, 7):
-            arrive(("core", g, s))
-        add_products(g, every, (0, 1, 7))
-    for s in (2, 6):
-        arrive(("core", "r", s))
-        square_sources(s)
+    z_step("r", 3, 0)
+    from_core(0, (0, 1, 7))
+    add_products(0, every, (0, 1, 7))
+    z_step("r", 3, 1)
+    from_core("r", (2, 6))
+    square_sources(2)
+    square_sources(6)
     make_kernels(every, (2, 6))
-    z_step("r", 3)
-    for g in groups:
-        for s in (2, 6):
-            arrive(("core", g, s))
-        add_products(g, every, (2, 6))
-    for s in (3, 5):
-        arrive(("core", "r", s))
-        square_sources(s)
+    z_step(0, 3, 0)
+    from_core(0, (2, 6))
+    add_products(0, every, (2, 6))
+    from_core("r", (3, 5))
+    square_sources(3)
+    square_sources(5)
+    z_step(0, 3, 1)
     make_kernels(every, (3, 5))
-    for g in groups:
-        z_step(g, 3)
-    z_step("r", 4)
-    for g in groups:
-        for s in (3, 5):
-            arrive(("core", g, s))
-        add_products(g, every, (3, 5))
-    arrive(("core", "r", 4))
+    z_step("r", 4, 0)
+    from_core(0, (3, 5))
+    add_products(0, every, (3, 5))
+    z_step(0, 4, 0)
+    from_core("r", (4,))
     square_sources(4)
     make_kernels(every, (4,))
-    for g in groups:
-        z_step(g, 4)
-
-    order = [(half, s) for s in (2, 1, 3, 0) for half in (0, 1)]
-    for g in groups:
-        arrive(("core", g, 4))
-        before = None
-        for tile in order + [None]:
-            if tile is not None:
-                last_product(g, *tile, (4,))
-            if before is not None:
-                first_send(g, *before)
-                first_send_plain(g, *before)
-            before = tile
-        before = None
-        for tile in order + [None]:
-            if tile is not None:
-                first_add(g, *tile)
-            if before is not None:
-                first_send_added(g, *before)
-            before = tile
-        before = None
-        for tile in order + [None]:
-            if tile is not None:
-                second_prepare(g, *tile)
-            if before is not None:
-                second_send(g, *before)
-            before = tile
-        for half in (0, 1):
-            second_add(g, half)
-        for half in (0, 1):
-            second_send_added(g, half)
-        for half in (0, 1):
-            second_result(g, half)
+    from_core(0, (4,))
+
+    def for_both(f, *args):
+        for half in both:
+            f(0, half, *args)
+
+    for s in (2, 1, 3, 0):
+        for_both(last_product, s, (4,))
+        for_both(first_send, s)
+    for_both(first_send_plain, 2)
+    for s in (2, 1, 3):
+        for_both(first_add, s)
+        for_both(first_send_added, s)
+    for_both(first_send_plain, 1)
+    for_both(first_send_plain, 3)
+    for_both(first_add, 0)
+    for_both(second_prepare, 2)
+    for_both(second_send, 2)
+    for_both(first_send_added, 0)
+    for_both(first_send_plain, 0)
+    for s in (1, 3):
+        for_both(second_prepare, s)
+        for_both(second_send, s)
+    for_both(second_add)
+    for_both(second_send_added)
+    for_both(second_prepare, 0)
+    for_both(second_result)
 
     for made in copies.values():
         made.wait_send()
@@ -429,7 +443,7 @@
 
 def local(particles, scores, power):
     return pl.pallas_call(
-        kernel,
+        scoped_kernel,
         out_shape=jax.ShapeDtypeStruct((ROWS, D), F32),
         in_specs=[
             pl.BlockSpec(memory_space=pl.ANY),
@@ -455,9 +469,6 @@
             pltpu.VMEM((GROUPS, 2, 6 * QUARTER, W), BF16),
             pltpu.VMEM((GROUPS, 2, 2 * QUARTER, W), BF16),
             pltpu.VMEM((GROUPS, 2, 4 * QUARTER, W), BF16),
-            pltpu.SemaphoreType.DMA((2,)),
-            pltpu.SemaphoreType.DMA((COPIES,)),
-            pltpu.SemaphoreType.DMA((COPIES,)),
         ],
         compiler_params=pltpu.CompilerParams(
             collective_id=0, has_side_effects=True, vmem_limit_bytes=56 * 2**20

time: 63.3 us -> 50.7 us (0.80)
  Pallas kernels: 61.5 us -> 48.9 us
    pallas_call x1, Pallas kernels: 61.5 us -> 48.9 us  [local(): pl.pallas_call(scoped_kernel, out_shape=jax.ShapeDtypeStruct((ROWS, D), F...]
where the time goes in v2:
time: 50.7 us; the launch traced here: 50.6 us
  Pallas kernels  48.9 us (96%)
  local copies, waits for them, and re-layouts  1.67 us (3%)
    pallas_call x1, Pallas kernels, local(): pl.pallas_call(scoped_kernel, out_shape=jax.ShapeDtypeStruct((ROWS, D), F...  48.9 us
    unnamed x1, local copies, waits for them, and re-layouts  1.67 us

profile of v2, /device:TPU:1, one launch (start us, length us, event | category | flops | bytes accessed | tf_op | source)
XLA Modules:
  0.0 50.6 jit_solution(7441217681952171672)
XLA Ops:
  0.0 48.9 %shard_map.37 = f32[128,512]{1,0:T(8,128)} custom-call(f32[128,512]{1,0:T(8,128)} %refs_0_.1, bf16[128,512]{1,0:T(8,128)(2,1)} %refs_1_.1, s32[1,512]{1,0:T(1,128)} %bitcast.1), custom_call_target="tpu_custom_call" | custom-call | tf_op jit(solution)/shard_map/pallas_call | solution.py:445
  48.9 1.7 %copy.5 = f32[128,512]{1,0:T(8,128)} copy(f32[128,512]{1,0:T(8,128)} %shard_map.37) | data formatting | bytes 524288

commit v3 on v2

--- a/solution.py
+++ b/solution.py
@@ -17,7 +17,7 @@
 HALF = ROWS // 2
 QUARTER = ROWS // 4
 TILE = 4 * HALF
-COPIES = 172
+COPIES = 170
 
 
 def neighbours():
@@ -33,21 +33,23 @@
         ids["x", step] = at((x + step + 4) % 4, y, gy, core)
         ids["y", step] = at(x, (y + step + 4) % 4, gy, core)
         ids["z", step] = at(x, y, (gy + step + 8) % 8, core)
+    ids["x", 2] = at((x + 2) % 4, y, gy, core)
+    ids["y", 2] = at(x, (y + 2) % 4, gy, core)
     return ids
 
 
 def scoped_kernel(*refs):
     pl.run_scoped(
         functools.partial(kernel, *refs),
-        pltpu.SemaphoreType.DMA((2,)),
+        pltpu.SemaphoreType.DMA((3,)),
         pltpu.SemaphoreType.DMA((COPIES,)),
         pltpu.SemaphoreType.DMA((COPIES,)),
     )
 
 
 def kernel(
-    particles_hbm, scores_hbm, power_ref, out_ref,
-    particles, scores, targets, sources, source_scores, kernels, acc,
+    particles_hbm, scores_hbm, power_hbm, out_ref,
+    particles, scores, power_ref, targets, sources, source_scores, kernels, acc,
     target_squares, source_squares, totals, inverse,
     sent, relay, arrived, sent2, relay2, arrived2,
     load_sem, send_sem, recv_sem,
@@ -55,6 +57,7 @@
     loads = [
         pltpu.make_async_copy(particles_hbm, particles, load_sem.at[0]),
         pltpu.make_async_copy(scores_hbm, scores, load_sem.at[1]),
+        pltpu.make_async_copy(power_hbm, power_ref, load_sem.at[2]),
     ]
     for load in loads:
         load.start()
@@ -78,19 +81,17 @@
     def arrive(name):
         copies[name].wait_recv()
 
-    weights = jnp.exp2(-power_ref[...].astype(F32))
     for load in loads:
         load.wait()
+    weights = jnp.exp2(-power_ref[...].astype(F32))
     rounded = particles[...].astype(BF16)
-    rounded_f = rounded.astype(F32)
-    double = rounded_f * (2.0 * weights)
+    double = rounded.astype(F32) * (2.0 * weights)
+    sources[0, 0] = double.T.astype(BF16)
     targets[0, 0, 0:HALF] = rounded[:HALF]
     targets[1, 0, 0:HALF] = rounded[HALF:]
-    sources[0, 0] = double.T.astype(BF16)
     folded = (scores[...].astype(F32) - double).astype(BF16)
     for g in range(GROUPS):
         source_scores[g, 0, 0:ROWS] = folded[:, g * W : (g + 1) * W]
-    inverse[...] = jnp.broadcast_to(0.25 / weights, (ROWS, D)).T
 
     pl.semaphore_wait(barrier, len(ids))
 
@@ -143,14 +144,13 @@
                 (axes[half][0], step),
             )
 
-    def t_first_relay(half):
-        for step, src, part in ((1, 3, 0), (-1, 1, QUARTER)):
-            copy(
-                ("c2", half, step),
-                targets.at[half, 0, pl.ds(src * HALF + part, QUARTER)],
-                targets.at[half, 0, pl.ds(2 * HALF + part, QUARTER)],
-                (axes[half][0], step),
-            )
+    def t_first_far(half):
+        copy(
+            ("c2", half),
+            targets.at[half, 0, pl.ds(0, HALF)],
+            targets.at[half, 0, pl.ds(2 * HALF, HALF)],
+            (axes[half][0], 2),
+        )
 
     def t_second(half, i):
         for step, land in ((1, 3), (-1, 1)):
@@ -322,23 +322,25 @@
         for half in both:
             t_first(half)
         for half in both:
+            t_first_far(half)
+        for half in both:
             t_second(half, 0)
         z_send("r", 0, 1)
         to_core("r", 0)
         z_send(0, 0, 0)
         z_send(0, 0, 1)
         to_core(0, 0)
+        inverse[...] = jnp.broadcast_to(0.25 / weights, (ROWS, D)).T
 
     def t_step1():
         t_arrive("c1")
-        for half in both:
-            t_first_relay(half)
         for i in (3, 1):
             for half in both:
                 t_second(half, i)
 
     def t_step2():
-        t_arrive("c2")
+        for half in both:
+            arrive(("c2", half))
         for half in both:
             t_second(half, 2)
         t_arrive("c3", 0)
@@ -360,26 +362,30 @@
     z_step("r", 1, 1)
     from_core("r", (0,))
     square_sources(0)
+    t_step2()
     z_step(0, 1, 0)
-    t_step2()
     for tile in near:
         square_targets(*tile)
     make_kernels(near, (0,))
-    z_step(0, 1, 1)
-    t_step3(3)
     from_core("r", (1, 7))
     square_sources(1)
     square_sources(7)
-    z_step("r", 2, 0)
+    z_step(0, 1, 1)
+    t_step3(3)
     t_step3(1)
     make_kernels(near, (1, 7))
-    z_step("r", 2, 1)
+    z_step("r", 2, 0)
     t_step3(2)
     for tile in middle:
         square_targets(*tile)
     make_kernels(middle, (0,))
+    z_step("r", 2, 1)
+    make_kernels(middle, (1, 7))
     z_step(0, 2, 0)
-    make_kernels(middle, (1, 7))
+    from_core("r", (2, 6))
+    square_sources(2)
+    square_sources(6)
+    make_kernels(near + middle, (2, 6))
     z_step(0, 2, 1)
     t_step4()
     for tile in far:
@@ -387,27 +393,24 @@
     make_kernels(far, (0, 1, 7))
     z_step("r", 3, 0)
     from_core(0, (0, 1, 7))
-    add_products(0, every, (0, 1, 7))
+    add_products(0, near + middle, (0, 1, 7))
     z_step("r", 3, 1)
-    from_core("r", (2, 6))
-    square_sources(2)
-    square_sources(6)
-    make_kernels(every, (2, 6))
+    make_kernels(far, (2, 6))
+    add_products(0, far, (0, 1, 7))
     z_step(0, 3, 0)
     from_core(0, (2, 6))
     add_products(0, every, (2, 6))
+    z_step(0, 3, 1)
     from_core("r", (3, 5))
     square_sources(3)
     square_sources(5)
-    z_step(0, 3, 1)
     make_kernels(every, (3, 5))
     z_step("r", 4, 0)
-    from_core(0, (3, 5))
-    add_products(0, every, (3, 5))
     z_step(0, 4, 0)
     from_core("r", (4,))
     square_sources(4)
     make_kernels(every, (4,))
+    from_core(0, (3, 5))
     from_core(0, (4,))
 
     def for_both(f, *args):
@@ -415,7 +418,7 @@
             f(0, half, *args)
 
     for s in (2, 1, 3, 0):
-        for_both(last_product, s, (4,))
+        for_both(last_product, s, (3, 5, 4))
         for_both(first_send, s)
     for_both(first_send_plain, 2)
     for s in (2, 1, 3):
@@ -446,14 +449,15 @@
         scoped_kernel,
         out_shape=jax.ShapeDtypeStruct((ROWS, D), F32),
         in_specs=[
-            pl.BlockSpec(memory_space=pl.ANY),
-            pl.BlockSpec(memory_space=pl.ANY),
-            pl.BlockSpec(memory_space=pltpu.VMEM),
+            pl.BlockSpec(memory_space=pltpu.HBM),
+            pl.BlockSpec(memory_space=pltpu.HBM),
+            pl.BlockSpec(memory_space=pltpu.HBM),
         ],
         out_specs=pl.BlockSpec(memory_space=pltpu.VMEM),
         scratch_shapes=[
             pltpu.VMEM((ROWS, D), F32),
             pltpu.VMEM((ROWS, D), BF16),
+            pltpu.VMEM((1, D), jnp.int32),
             pltpu.VMEM((2, 4, TILE, D), BF16),
             pltpu.VMEM((8, 2, D, ROWS), BF16),
             pltpu.VMEM((GROUPS, 8, 2 * ROWS, W), BF16),
@@ -471,9 +475,9 @@
             pltpu.VMEM((GROUPS, 2, 4 * QUARTER, W), BF16),
         ],
         compiler_params=pltpu.CompilerParams(
-            collective_id=0, has_side_effects=True, vmem_limit_bytes=56 * 2**20
+            collective_id=0, has_side_effects=True, vmem_limit_bytes=30 * 2**20
         ),
-    )(particles, scores, power.reshape(1, D))
+    )(*[pltpu.with_memory_space_constraint(a, pltpu.HBM) for a in (particles, scores, power.reshape(1, D))])
 
 
 def solution(mesh):

time: 50.7 us -> 47.9 us (0.945)
  Pallas kernels: 48.9 us -> 47.1 us
  local copies, waits for them, and re-layouts: 1.67 us -> 0.71 us
    pallas_call x1, Pallas kernels: 48.9 us -> 47.1 us  [local(): pl.pallas_call(scoped_kernel, out_shape=jax.ShapeDtypeStruct((ROWS, D), F...]
    unnamed x1, local copies, waits for them, and re-layouts: 1.67 us -> 0.71 us
where the time goes in v3:
time: 47.9 us; the launch traced here: 47.8 us
  Pallas kernels  47.1 us (98%)
  local copies, waits for them, and re-layouts  0.71 us (1%)
    pallas_call x1, Pallas kernels, local(): pl.pallas_call(scoped_kernel, out_shape=jax.ShapeDtypeStruct((ROWS, D), F...  47.1 us

profile of v3, /device:TPU:1, one launch (start us, length us, event | category | flops | bytes accessed | tf_op | source)
XLA Modules:
  0.0 47.8 jit_solution(13874465542336376631)
XLA Ops:
  0.0 47.1 %shard_map.37 = f32[128,512]{1,0:T(8,128)S(1)} custom-call(f32[128,512]{1,0:T(8,128)} %refs_0_.1, bf16[128,512]{1,0:T(8,128)(2,1)} %refs_1_.1, s32[1,512]{1,0:T(1,128)} %bitcast.1), custom_call_target="tpu_custom_call" | custom-call | tf_op jit(solution)/shard_map/pallas_call | solution.py:448
  47.1 0.7 %copy.5 = f32[128,512]{1,0:T(8,128)} copy(f32[128,512]{1,0:T(8,128)S(1)} %shard_map.37) | data formatting | bytes 524288

commit v4 on v3

v4 whole, which is shorter than its diff:
```python
import functools

import jax
import jax.numpy as jnp
from jax import lax
from jax.experimental import pallas as pl
from jax.experimental.pallas import tpu as pltpu
from jax.sharding import PartitionSpec as P

F32 = jnp.float32
BF16 = jnp.bfloat16
LOG2E = 1.4426950408889634
ROWS = 128
D = 512
W = D // 2
HALF = ROWS // 2
QUARTER = ROWS // 4
TILE = 4 * HALF
COPIES = 196


def neighbours():
    gx, gy, gz = lax.axis_index("gx"), lax.axis_index("gy"), lax.axis_index("gz")
    y_hi, x, core = gx // 8, (gx // 2) % 4, gx % 2
    y = y_hi * 2 + gz

    def at(x, y, z, core):
        return {"gx": (y // 2) * 8 + x * 2 + core, "gy": z, "gz": y % 2}

    ids = {"core": at(x, y, gy, 1 - core)}
    for step in (1, -1):
        ids["x", step] = at((x + step + 4) % 4, y, gy, core)
        ids["y", step] = at(x, (y + step + 4) % 4, gy, core)
        ids["z", step] = at(x, y, (gy + step + 8) % 8, core)
    ids["x", 2] = at((x + 2) % 4, y, gy, core)
    ids["y", 2] = at(x, (y + 2) % 4, gy, core)
    ids["z", 2] = at(x, y, (gy + 2) % 8, core)
    ids["z", -2] = at(x, y, (gy + 6) % 8, core)
    return ids


def scoped_kernel(*refs):
    pl.run_scoped(
        functools.partial(kernel, *refs),
        pltpu.SemaphoreType.DMA((3,)),
        pltpu.SemaphoreType.DMA((COPIES,)),
        pltpu.SemaphoreType.DMA((COPIES,)),
    )


def kernel(
    particles_hbm, scores_hbm, power_hbm, out_ref,
    particles, scores, power_ref, targets, target_scores, sources, source_scores, kernels, acc,
    target_squares, source_squares, totals, inverse, turned,
    sent, relay, arrived, sent2, relay2, arrived2, back, gave, got, back_sent, back_came,
    load_sem, send_sem, recv_sem,
):
    loads = [
        pltpu.make_async_copy(particles_hbm, particles, load_sem.at[0]),
        pltpu.make_async_copy(scores_hbm, scores, load_sem.at[1]),
        pltpu.make_async_copy(power_hbm, power_ref, load_sem.at[2]),
    ]
    for load in loads:
        load.start()
    ids = neighbours()
    barrier = pltpu.get_barrier_semaphore()
    for device in ids.values():
        pl.semaphore_signal(barrier, inc=1, device_id=device, device_id_type=pl.DeviceIdType.MESH)

    copies = {}

    def copy(name, src, dst, device):
        n = len(copies)
        made = pltpu.make_async_remote_copy(
            src_ref=src, dst_ref=dst, send_sem=send_sem.at[n], recv_sem=recv_sem.at[n],
            device_id=ids[device], device_id_type=pl.DeviceIdType.MESH,
        )
        assert name not in copies
        copies[name] = made
        made.start()

    def arrive(name):
        copies[name].wait_recv()

    for load in loads:
        load.wait()
    weights = jnp.exp2(-power_ref[...].astype(F32))
    rounded = particles[...].astype(BF16)
    double = rounded.astype(F32) * (2.0 * weights)
    sources[0, 0] = double.T.astype(BF16)
    targets[0, 0, 0:HALF] = rounded[:HALF]
    targets[1, 0, 0:HALF] = rounded[HALF:]
    folded = (scores[...].astype(F32) - double).astype(BF16)
    source_scores[0, 0:ROWS] = folded[:, :W]
    target_scores[0, 0, 0:HALF] = folded[:HALF, W:]
    target_scores[1, 0, 0:HALF] = folded[HALF:, W:]

    pl.semaphore_wait(barrier, len(ids))

    def slot(step, h):
        return h if step == 1 else 8 - h

    def piece(size, step, n):
        first = 0 if step == 1 else 1
        return pl.ds((first + n) % 2 * (size // 2), size // 2)

    def z_send(kind, h, n):
        for step in (1, -1):
            src, dst = slot(step, h) % 8, slot(step, h + 1)
            if kind == "r":
                rows = piece(D, step, n)
                a, b = sources.at[src, 0, rows], sources.at[dst, 0, rows]
            else:
                rows = piece(ROWS, step, 0) if h == 3 else pl.ds(0, ROWS)
                a, b = source_scores.at[src, rows], source_scores.at[dst, rows]
            copy(("z", kind, h + 1, n, step), a, b, ("z", step))

    def to_core(kind, s):
        if kind == "r":
            copy(("core", kind, s), sources.at[s, 0], sources.at[s, 1], "core")
        else:
            block = source_scores.at[s]
            copy(("core", kind, s), block.at[pl.ds(0, ROWS)], block.at[pl.ds(ROWS, ROWS)], "core")

    def z_step(kind, h, n=0):
        for step in (1, -1):
            arrive(("z", kind, h, n, step))
        if h < 3 or (h == 3 and n == 0):
            z_send(kind, h, n)
        if n == 1 or h == 4 or kind == "s":
            for s in sorted({h, 8 - h}):
                to_core(kind, s)

    axes = (("x", "y"), ("y", "x"))

    def t_first(ref, half):
        for step, land in ((1, 3), (-1, 1)):
            copy(
                ("c1", ref is targets, half, step),
                ref.at[half, 0, pl.ds(0, HALF)],
                ref.at[half, 0, pl.ds(land * HALF, HALF)],
                (axes[half][0], step),
            )

    def t_first_far(ref, half):
        copy(
            ("c2", ref is targets, half),
            ref.at[half, 0, pl.ds(0, HALF)],
            ref.at[half, 0, pl.ds(2 * HALF, HALF)],
            (axes[half][0], 2),
        )

    def t_second(ref, half, i):
        for step, land in ((1, 3), (-1, 1)):
            copy(
                ("c3", ref is targets, half, i, step),
                ref.at[half, 0, pl.ds(i * HALF, HALF)],
                ref.at[half, land, pl.ds(i * HALF, HALF)],
                (axes[half][1], step),
            )

    def t_second_relay(ref, half, i):
        for step, src, part in ((1, 3, 0), (-1, 1, QUARTER)):
            copy(
                ("c6", ref is targets, half, i, step),
                ref.at[half, src, pl.ds(i * HALF + part, QUARTER)],
                ref.at[half, 2, pl.ds(i * HALF + part, QUARTER)],
                (axes[half][1], step),
            )

    def t_arrive(name, ref, *at):
        for half in (0, 1):
            for step in (1, -1):
                arrive((name, ref is targets, half, *at, step))

    def t_start(ref):
        for half in (0, 1):
            t_first(ref, half)
        for half in (0, 1):
            t_first_far(ref, half)
        for half in (0, 1):
            t_second(ref, half, 0)

    def t_step1(ref):
        t_arrive("c1", ref)
        for i in (3, 1):
            for half in (0, 1):
                t_second(ref, half, i)

    def t_step2(ref):
        for half in (0, 1):
            arrive(("c2", ref is targets, half))
        for half in (0, 1):
            t_second(ref, half, 2)
        t_arrive("c3", ref, 0)
        for half in (0, 1):
            t_second_relay(ref, half, 0)

    def t_step3(ref, i):
        t_arrive("c3", ref, i)
        for half in (0, 1):
            t_second_relay(ref, half, i)

    def t_step4(ref):
        for i in range(4):
            t_arrive("c6", ref, i)

    def square_targets(tiles):
        for half, s in tiles:
            rows = targets[half, s].astype(F32)
            total = jnp.sum(rows * rows * weights, axis=1, keepdims=True) * LOG2E
            target_squares[half, s] = jnp.broadcast_to(total, (TILE, 128))

    def square_sources(s):
        for core in (0, 1):
            part = sources[s, core].astype(F32)
            total = jnp.sum(part * part * inverse[...], axis=0, keepdims=True) * LOG2E
            source_squares[s, :, core * 128 : core * 128 + 128] = total

    def make_kernels(tiles, slots):
        for tile in tiles:
            for k in slots:
                both = jnp.concatenate([sources[k, 0], sources[k, 1]], axis=1)
                inner = jnp.dot(targets[tile], both, preferred_element_type=F32)
                own = target_squares[tile]
                power = inner * LOG2E - jnp.concatenate([own, own], axis=1) - source_squares[k]
                values = jnp.exp2(power).astype(BF16)
                kernels[(*tile, k)] = values
                values = values.astype(F32)
                pair = values[:, :128] + values[:, 128:]
                if k == 0:
                    totals[tile] = pair
                else:
                    totals[tile] += pair

    def product(half, s, slots):
        left = jnp.concatenate([kernels[half, s, k] for k in slots], axis=1)
        right = jnp.concatenate([source_scores[k] for k in slots], axis=0)
        return jnp.dot(left, right, preferred_element_type=F32)

    def last_product(half, s, slots):
        row_totals = jnp.sum(totals[half, s], axis=1, keepdims=True)
        rows = targets[half, s, :, 0:W].astype(F32)
        result = product(half, s, slots) + rows * (2.0 * weights[:, :W]) * row_totals
        acc[half, s] = result
        sent[half, s, 0:HALF] = result[2 * HALF : 3 * HALF].astype(BF16)
        sent[half, s, HALF : HALF + QUARTER] = result[HALF + QUARTER : 2 * HALF].astype(BF16)
        sent[half, s, HALF + QUARTER : TILE // 2] = result[3 * HALF : 3 * HALF + QUARTER].astype(BF16)

    def turn(tiles):
        for half, s in tiles:
            n = (half * 4 + s) * TILE
            turned[0:W, n : n + TILE] = target_scores[half, s].T

    def back_product(k):
        right = jnp.concatenate([kernels[half, s, k] for half in (0, 1) for s in range(4)], axis=0)
        rows = jnp.concatenate([sources[k, 0, W:], sources[k, 1, W:]], axis=1).astype(F32)
        result = jnp.dot(turned[...], right, preferred_element_type=F32)
        result = result[:W] + rows * result[W : W + 1]
        back[k] = result[:, :ROWS]
        gave[k] = result[:, ROWS:].astype(BF16)

    def give(k):
        copy(("give", k), gave.at[k], got.at[k], "core")

    def take(k):
        arrive(("give", k))
        back[k] += got[k].astype(F32)

    def back_rows(step, part):
        return pl.ds(part * ROWS if step == 1 else (1 - part) * ROWS, ROWS)

    def back_message(h, part):
        came = {(2, 0): ((4, 0), (3, 0)), (1, 0): ((2, 0),), (2, 1): ((3, 1),), (1, 1): ((2, 1),)}
        for n, step in enumerate((1, -1)):
            value = back[slot(step, h), back_rows(step, part)]
            for at in came.get((h, part), ()):
                arrive(("back", *at, step))
                value += back_came[(n, *at)].astype(F32)
            back_sent[n, h, part] = value.astype(BF16)

    def back_send(h, part):
        for n, step in enumerate((1, -1)):
            copy(
                ("back", h, part, step),
                back_sent.at[n, h, part],
                back_came.at[n, h, part],
                ("z", -2 * step if h == 4 else -step),
            )

    def back_result():
        for part in (0, 1):
            for n, step in enumerate((1, -1)):
                arrive(("back", 1, part, step))
                back[0, back_rows(step, part)] += back_came[n, 1, part].astype(F32)
        out_ref[:, W:] = back[0].T

    def q4(n):
        return pl.ds(n * QUARTER, QUARTER)

    def first_send(half, s):
        axis = axes[half][0]
        base = sent.at[half, s]
        copy(("rel", half, s, 1), base.at[q4(0)], relay.at[half, s, q4(0)], (axis, 1))
        copy(("rel", half, s, -1), base.at[q4(1)], relay.at[half, s, q4(1)], (axis, -1))

    def first_send_plain(half, s):
        axis = axes[half][0]
        base = sent.at[half, s]
        copy(("pln", half, s, 1), base.at[q4(2)], arrived.at[half, s, q4(1)], (axis, 1))
        copy(("pln", half, s, -1), base.at[q4(3)], arrived.at[half, s, q4(2)], (axis, -1))

    def first_add(half, s):
        for step in (1, -1):
            arrive(("rel", half, s, step))
        summed = acc[half, s, pl.ds(HALF, QUARTER)] + relay[half, s, q4(0)].astype(F32)
        sent[half, s, q4(4)] = summed.astype(BF16)
        summed = acc[half, s, pl.ds(3 * HALF + QUARTER, QUARTER)] + relay[half, s, q4(1)].astype(F32)
        sent[half, s, q4(5)] = summed.astype(BF16)

    def first_send_added(half, s):
        axis = axes[half][0]
        base = sent.at[half, s]
        copy(("add", half, s, 1), base.at[q4(4)], arrived.at[half, s, q4(0)], (axis, 1))
        copy(("add", half, s, -1), base.at[q4(5)], arrived.at[half, s, q4(3)], (axis, -1))

    def first_result(half, s):
        for name in ("pln", "add"):
            for step in (1, -1):
                arrive((name, half, s, step))
        own = acc[half, s, pl.ds(0, HALF)]
        came = arrived[half, s].astype(F32)
        return own + came[:HALF] + came[HALF:]

    def second_prepare(half, s):
        result = first_result(half, s)
        if s == 2:
            sent2[half, pl.ds(0, HALF)] = result.astype(BF16)
        elif s == 1:
            sent2[half, q4(2)] = result[QUARTER:].astype(BF16)
            acc[half, 1, pl.ds(0, QUARTER)] = result[:QUARTER]
        elif s == 3:
            sent2[half, q4(3)] = result[:QUARTER].astype(BF16)
            acc[half, 3, pl.ds(0, QUARTER)] = result[QUARTER:]
        else:
            acc[half, 0, pl.ds(0, HALF)] = result

    def second_send(half, s):
        axis = axes[half][1]
        base = sent2.at[half]
        if s == 2:
            copy(("rel2", half, 1), base.at[q4(0)], relay2.at[half, q4(0)], (axis, 1))
            copy(("rel2", half, -1), base.at[q4(1)], relay2.at[half, q4(1)], (axis, -1))
        elif s == 1:
            copy(("pln2", half, 1), base.at[q4(2)], arrived2.at[half, q4(1)], (axis, 1))
        elif s == 3:
            copy(("pln2", half, -1), base.at[q4(3)], arrived2.at[half, q4(2)], (axis, -1))

    def second_add(half):
        for step in (1, -1):
            arrive(("rel2", half, step))
        summed = acc[half, 1, pl.ds(0, QUARTER)] + relay2[half, q4(0)].astype(F32)
        sent2[half, q4(4)] = summed.astype(BF16)
        summed = acc[half, 3, pl.ds(0, QUARTER)] + relay2[half, q4(1)].astype(F32)
        sent2[half, q4(5)] = summed.astype(BF16)

    def second_send_added(half):
        axis = axes[half][1]
        base = sent2.at[half]
        copy(("add2", half, 1), base.at[q4(4)], arrived2.at[half, q4(0)], (axis, 1))
        copy(("add2", half, -1), base.at[q4(5)], arrived2.at[half, q4(3)], (axis, -1))

    def second_result(half):
        for name in ("pln2", "add2"):
            for step in (1, -1):
                arrive((name, half, step))
        came = arrived2[half].astype(F32)
        result = acc[half, 0, pl.ds(0, HALF)] + came[:HALF] + came[HALF:]
        out_ref[half * HALF : half * HALF + HALF, 0:W] = result

    near = [(0, 0), (1, 0)]
    middle = [(half, s) for s in (1, 3) for half in (0, 1)]
    far = [(0, 2), (1, 2)]
    every = near + middle + far

    def from_core(kind, slots):
        for s in slots:
            arrive(("core", kind, s))
        if kind == "r":
            for s in slots:
                square_sources(s)

    def for_both(f, *args):
        for half in (0, 1):
            f(half, *args)

    def start():
        z_send("r", 0, 0)
        t_start(targets)
        z_send("r", 0, 1)
        to_core("r", 0)
        z_send("s", 0, 0)
        to_core("s", 0)
        inverse[...] = jnp.broadcast_to(0.25 / weights, (ROWS, D)).T
        turned[W:] = jnp.ones((16, 8 * TILE), BF16)

    start()
    t_step1(targets)
    z_step("r", 1, 0)
    z_step("r", 1, 1)
    from_core("r", (0,))
    t_step2(targets)
    t_start(target_scores)
    z_step("s", 1)
    square_targets(near)
    from_core("r", (1, 7))
    make_kernels(near, (0, 1, 7))
    z_step("r", 2, 0)
    t_step3(targets, 3)
    z_step("r", 2, 1)
    t_step3(targets, 1)
    z_step("s", 2)
    t_step3(targets, 2)
    square_targets(middle)
    make_kernels(middle, (0, 1))
    z_step("r", 3, 0)
    t_step1(target_scores)
    make_kernels(middle, (7,))
    z_step("r", 3, 1)
    t_step2(target_scores)
    from_core("r", (2, 6))
    make_kernels(near + middle, (2, 6))
    z_step("s", 3)
    t_step4(targets)
    square_targets(far)
    make_kernels(far, (0, 1, 7, 2, 6))
    t_step3(target_scores, 3)
    t_step3(target_scores, 1)
    z_step("r", 4)
    from_core("r", (3, 5))
    make_kernels(every, (3, 5))
    t_step3(target_scores, 2)
    z_step("s", 4)
    from_core("r", (4,))
    from_core("s", (0, 1, 7, 2, 6, 3, 5))
    make_kernels(every, (4,))
    slots = (0, 1, 7, 2, 6, 3, 5, 4)
    from_core("s", (4,))
    for_both(last_product, 2, slots)
    t_step4(target_scores)
    for_both(first_send, 2)
    for_both(first_send_plain, 2)
    turn(every)
    for k in (4, 3, 5):
        back_product(k)
    for k in (4, 3, 5):
        give(k)
    for s in (1, 3):
        for_both(last_product, s, slots)
    for s in (1, 3):
        for_both(first_send, s)
    for k in (4, 3, 5):
        take(k)
    back_message(3, 0)
    back_message(4, 0)
    back_message(3, 1)
    for_both(first_add, 2)
    back_send(3, 0)
    back_send(4, 0)
    back_send(3, 1)
    for_both(first_send_added, 2)
    for_both(last_product, 0, slots)
    for k in (2, 6):
        back_product(k)
    give(2)
    give(6)
    for_both(first_send, 0)
    for s in (1, 3):
        for_both(first_add, s)
        for_both(first_send_added, s)
        for_both(first_send_plain, s)
    for k in (1, 7, 0):
        back_product(k)
    for k in (1, 7, 0):
        give(k)
    take(2)
    take(6)
    for_both(second_prepare, 2)
    for_both(second_send, 2)
    back_message(2, 0)
    back_message(2, 1)
    back_send(2, 0)
    back_send(2, 1)
    for_both(first_add, 0)
    for_both(first_send_added, 0)
    for_both(first_send_plain, 0)
    for k in (1, 7, 0):
        take(k)
    for s in (1, 3):
        for_both(second_prepare, s)
        for_both(second_send, s)
    for_both(second_add)
    for_both(second_send_added)
    back_message(1, 0)
    back_message(1, 1)
    back_send(1, 0)
    back_send(1, 1)
    for_both(second_prepare, 0)
    for_both(second_result)
    back_result()

    for made in copies.values():
        made.wait_send()
    assert len(copies) <= COPIES


def local(particles, scores, power):
    return pl.pallas_call(
        scoped_kernel,
        out_shape=jax.ShapeDtypeStruct((ROWS, D), F32),
        in_specs=[
            pl.BlockSpec(memory_space=pltpu.HBM),
            pl.BlockSpec(memory_space=pltpu.HBM),
            pl.BlockSpec(memory_space=pltpu.HBM),
        ],
        out_specs=pl.BlockSpec(memory_space=pltpu.VMEM),
        scratch_shapes=[
            pltpu.VMEM((ROWS, D), F32),
            pltpu.VMEM((ROWS, D), BF16),
            pltpu.VMEM((1, D), jnp.int32),
            pltpu.VMEM((2, 4, TILE, D), BF16),
            pltpu.VMEM((2, 4, TILE, W), BF16),
            pltpu.VMEM((8, 2, D, ROWS), BF16),
            pltpu.VMEM((8, 2 * ROWS, W), BF16),
            pltpu.VMEM((2, 4, 8, TILE, 2 * ROWS), BF16),
            pltpu.VMEM((2, 4, TILE, W), F32),
            pltpu.VMEM((2, 4, TILE, 128), F32),
            pltpu.VMEM((8, 1, 2 * ROWS), F32),
            pltpu.VMEM((2, 4, TILE, 128), F32),
            pltpu.VMEM((D, ROWS), F32),
            pltpu.VMEM((W + 16, 8 * TILE), BF16),
            pltpu.VMEM((2, 4, 6 * QUARTER, W), BF16),
            pltpu.VMEM((2, 4, 2 * QUARTER, W), BF16),
            pltpu.VMEM((2, 4, 4 * QUARTER, W), BF16),
            pltpu.VMEM((2, 6 * QUARTER, W), BF16),
            pltpu.VMEM((2, 2 * QUARTER, W), BF16),
            pltpu.VMEM((2, 4 * QUARTER, W), BF16),
            pltpu.VMEM((8, W, ROWS), F32),
            pltpu.VMEM((8, W, ROWS), BF16),
            pltpu.VMEM((8, W, ROWS), BF16),
            pltpu.VMEM((2, 5, 2, ROWS, ROWS), BF16),
            pltpu.VMEM((2, 5, 2, ROWS, ROWS), BF16),
        ],
        compiler_params=pltpu.CompilerParams(
            collective_id=0, has_side_effects=True, vmem_limit_bytes=30 * 2**20
        ),
    )(*[pltpu.with_memory_space_constraint(a, pltpu.HBM) for a in (particles, scores, power.reshape(1, D))])


def solution(mesh):
    split = P(("gx", "gy", "gz"), None)
    return jax.shard_map(
        local, mesh=mesh, in_specs=(split, split, P()), out_specs=split, check_vma=False
    )
```

time: 47.9 us -> 47.9 us (level)
  the two profiles are of different devices: /device:TPU:1 before, /device:TPU:2 now
where the time goes in v4:
time: 47.9 us; the launch traced here: 47.8 us
  Pallas kernels  47.1 us (98%)
  local copies, waits for them, and re-layouts  0.71 us (1%)
    pallas_call x1, Pallas kernels, local(): pl.pallas_call(scoped_kernel, out_shape=jax.ShapeDtypeStruct((ROWS, D), F...  47.1 us

profile of v4, /device:TPU:2, one launch (start us, length us, event | category | flops | bytes accessed | tf_op | source)
XLA Modules:
  0.0 47.8 jit_solution(1658325408438419238)
XLA Ops:
  0.0 47.1 %shard_map.37 = f32[128,512]{1,0:T(8,128)S(1)} custom-call(f32[128,512]{1,0:T(8,128)} %refs_0_.1, bf16[128,512]{1,0:T(8,128)(2,1)} %refs_1_.1, s32[1,512]{1,0:T(1,128)} %bitcast.1), custom_call_target="tpu_custom_call" | custom-call | tf_op jit(solution)/shard_map/pallas_call | solution.py:518
  47.1 0.7 %copy.5 = f32[128,512]{1,0:T(8,128)} copy(f32[128,512]{1,0:T(8,128)S(1)} %shard_map.37) | data formatting | bytes 524288

commit v5 on v4

--- a/solution.py
+++ b/solution.py
@@ -16,7 +16,7 @@
 HALF = ROWS // 2
 QUARTER = ROWS // 4
 TILE = 4 * HALF
-COPIES = 196
+COPIES = 192
 
 
 def neighbours():
@@ -52,7 +52,7 @@
     particles_hbm, scores_hbm, power_hbm, out_ref,
     particles, scores, power_ref, targets, target_scores, sources, source_scores, kernels, acc,
     target_squares, source_squares, totals, inverse, turned,
-    sent, relay, arrived, sent2, relay2, arrived2, back, gave, got, back_sent, back_came,
+    sent, relay, arrived, sent2, arrived2, back, gave, got, back_sent, back_came,
     load_sem, send_sem, recv_sem,
 ):
     loads = [
@@ -144,11 +144,20 @@
 
     def t_first_far(ref, half):
         copy(
-            ("c2", ref is targets, half),
+            ("c2", half),
             ref.at[half, 0, pl.ds(0, HALF)],
             ref.at[half, 0, pl.ds(2 * HALF, HALF)],
             (axes[half][0], 2),
         )
+
+    def t_first_relay(ref, half):
+        for step, src, part in ((1, 3, 0), (-1, 1, QUARTER)):
+            copy(
+                ("c2", half, step),
+                ref.at[half, 0, pl.ds(src * HALF + part, QUARTER)],
+                ref.at[half, 0, pl.ds(2 * HALF + part, QUARTER)],
+                (axes[half][0], step),
+            )
 
     def t_second(ref, half, i):
         for step, land in ((1, 3), (-1, 1)):
@@ -176,25 +185,30 @@
     def t_start(ref):
         for half in (0, 1):
             t_first(ref, half)
-        for half in (0, 1):
-            t_first_far(ref, half)
+        if ref is targets:
+            for half in (0, 1):
+                t_first_far(ref, half)
         for half in (0, 1):
             t_second(ref, half, 0)
 
     def t_step1(ref):
         t_arrive("c1", ref)
+        if ref is target_scores:
+            for half in (0, 1):
+                t_first_relay(ref, half)
         for i in (3, 1):
             for half in (0, 1):
                 t_second(ref, half, i)
 
     def t_step2(ref):
         for half in (0, 1):
-            arrive(("c2", ref is targets, half))
+            if ref is targets:
+                arrive(("c2", half))
+            else:
+                arrive(("c2", half, 1))
+                arrive(("c2", half, -1))
         for half in (0, 1):
             t_second(ref, half, 2)
-        t_arrive("c3", ref, 0)
-        for half in (0, 1):
-            t_second_relay(ref, half, 0)
 
     def t_step3(ref, i):
         t_arrive("c3", ref, i)
@@ -271,10 +285,10 @@
         return pl.ds(part * ROWS if step == 1 else (1 - part) * ROWS, ROWS)
 
     def back_message(h, part):
-        came = {(2, 0): ((4, 0), (3, 0)), (1, 0): ((2, 0),), (2, 1): ((3, 1),), (1, 1): ((2, 1),)}
+        came = ([(4, 0), (3, 0)], [(3, 1)])[part] if h == 2 else []
         for n, step in enumerate((1, -1)):
             value = back[slot(step, h), back_rows(step, part)]
-            for at in came.get((h, part), ()):
+            for at in came:
                 arrive(("back", *at, step))
                 value += back_came[(n, *at)].astype(F32)
             back_sent[n, h, part] = value.astype(BF16)
@@ -285,14 +299,15 @@
                 ("back", h, part, step),
                 back_sent.at[n, h, part],
                 back_came.at[n, h, part],
-                ("z", -2 * step if h == 4 else -step),
+                ("z", -step if h % 2 else -2 * step),
             )
 
     def back_result():
-        for part in (0, 1):
-            for n, step in enumerate((1, -1)):
-                arrive(("back", 1, part, step))
-                back[0, back_rows(step, part)] += back_came[n, 1, part].astype(F32)
+        for h in (1, 2):
+            for part in (0, 1):
+                for n, step in enumerate((1, -1)):
+                    arrive(("back", h, part, step))
+                    back[0, back_rows(step, part)] += back_came[n, h, part].astype(F32)
         out_ref[:, W:] = back[0].T
 
     def q4(n):
@@ -334,48 +349,24 @@
 
     def second_prepare(half, s):
         result = first_result(half, s)
-        if s == 2:
-            sent2[half, pl.ds(0, HALF)] = result.astype(BF16)
-        elif s == 1:
-            sent2[half, q4(2)] = result[QUARTER:].astype(BF16)
-            acc[half, 1, pl.ds(0, QUARTER)] = result[:QUARTER]
-        elif s == 3:
-            sent2[half, q4(3)] = result[:QUARTER].astype(BF16)
-            acc[half, 3, pl.ds(0, QUARTER)] = result[QUARTER:]
+        if s == 0:
+            acc[half, 0, pl.ds(0, HALF)] = result
         else:
-            acc[half, 0, pl.ds(0, HALF)] = result
+            sent2[half, s - 1] = result.astype(BF16)
 
     def second_send(half, s):
-        axis = axes[half][1]
-        base = sent2.at[half]
-        if s == 2:
-            copy(("rel2", half, 1), base.at[q4(0)], relay2.at[half, q4(0)], (axis, 1))
-            copy(("rel2", half, -1), base.at[q4(1)], relay2.at[half, q4(1)], (axis, -1))
-        elif s == 1:
-            copy(("pln2", half, 1), base.at[q4(2)], arrived2.at[half, q4(1)], (axis, 1))
-        elif s == 3:
-            copy(("pln2", half, -1), base.at[q4(3)], arrived2.at[half, q4(2)], (axis, -1))
-
-    def second_add(half):
-        for step in (1, -1):
-            arrive(("rel2", half, step))
-        summed = acc[half, 1, pl.ds(0, QUARTER)] + relay2[half, q4(0)].astype(F32)
-        sent2[half, q4(4)] = summed.astype(BF16)
-        summed = acc[half, 3, pl.ds(0, QUARTER)] + relay2[half, q4(1)].astype(F32)
-        sent2[half, q4(5)] = summed.astype(BF16)
-
-    def second_send_added(half):
-        axis = axes[half][1]
-        base = sent2.at[half]
-        copy(("add2", half, 1), base.at[q4(4)], arrived2.at[half, q4(0)], (axis, 1))
-        copy(("add2", half, -1), base.at[q4(5)], arrived2.at[half, q4(3)], (axis, -1))
+        copy(
+            ("sum2", half, s),
+            sent2.at[half, s - 1],
+            arrived2.at[half, s - 1],
+            (axes[half][1], (1, 2, -1)[s - 1]),
+        )
 
     def second_result(half):
-        for name in ("pln2", "add2"):
-            for step in (1, -1):
-                arrive((name, half, step))
-        came = arrived2[half].astype(F32)
-        result = acc[half, 0, pl.ds(0, HALF)] + came[:HALF] + came[HALF:]
+        result = acc[half, 0, pl.ds(0, HALF)]
+        for s in (1, 3, 2):
+            arrive(("sum2", half, s))
+            result += arrived2[half, s - 1].astype(F32)
         out_ref[half * HALF : half * HALF + HALF, 0:W] = result
 
     near = [(0, 0), (1, 0)]
@@ -399,6 +390,7 @@
         t_start(targets)
         z_send("r", 0, 1)
         to_core("r", 0)
+        t_start(target_scores)
         z_send("s", 0, 0)
         to_core("s", 0)
         inverse[...] = jnp.broadcast_to(0.25 / weights, (ROWS, D)).T
@@ -407,11 +399,12 @@
     start()
     t_step1(targets)
     z_step("r", 1, 0)
+    t_step2(targets)
     z_step("r", 1, 1)
     from_core("r", (0,))
-    t_step2(targets)
-    t_start(target_scores)
+    t_step3(targets, 0)
     z_step("s", 1)
+    t_step1(target_scores)
     square_targets(near)
     from_core("r", (1, 7))
     make_kernels(near, (0, 1, 7))
@@ -421,25 +414,25 @@
     t_step3(targets, 1)
     z_step("s", 2)
     t_step3(targets, 2)
+    t_step3(target_scores, 0)
     square_targets(middle)
     make_kernels(middle, (0, 1))
     z_step("r", 3, 0)
-    t_step1(target_scores)
+    t_step2(target_scores)
     make_kernels(middle, (7,))
     z_step("r", 3, 1)
-    t_step2(target_scores)
+    t_step3(target_scores, 3)
+    t_step3(target_scores, 1)
     from_core("r", (2, 6))
     make_kernels(near + middle, (2, 6))
     z_step("s", 3)
     t_step4(targets)
     square_targets(far)
     make_kernels(far, (0, 1, 7, 2, 6))
-    t_step3(target_scores, 3)
-    t_step3(target_scores, 1)
     z_step("r", 4)
+    t_step3(target_scores, 2)
     from_core("r", (3, 5))
     make_kernels(every, (3, 5))
-    t_step3(target_scores, 2)
     z_step("s", 4)
     from_core("r", (4,))
     from_core("s", (0, 1, 7, 2, 6, 3, 5))
@@ -457,52 +450,50 @@
         give(k)
     for s in (1, 3):
         for_both(last_product, s, slots)
+    for k in (4, 3, 5):
+        take(k)
+    back_message(4, 0)
+    back_message(3, 0)
+    back_message(3, 1)
     for s in (1, 3):
         for_both(first_send, s)
-    for k in (4, 3, 5):
-        take(k)
-    back_message(3, 0)
-    back_message(4, 0)
-    back_message(3, 1)
     for_both(first_add, 2)
+    back_send(4, 0)
     back_send(3, 0)
-    back_send(4, 0)
     back_send(3, 1)
     for_both(first_send_added, 2)
+    for s in (1, 3):
+        for_both(first_send_plain, s)
     for_both(last_product, 0, slots)
     for k in (2, 6):
         back_product(k)
-    give(2)
-    give(6)
     for_both(first_send, 0)
-    for s in (1, 3):
-        for_both(first_add, s)
-        for_both(first_send_added, s)
-        for_both(first_send_plain, s)
+    for k in (2, 6):
+        give(k)
     for k in (1, 7, 0):
         back_product(k)
     for k in (1, 7, 0):
         give(k)
+    for s in (1, 3):
+        for_both(first_add, s)
+        for_both(first_send_added, s)
+    for_both(first_send_plain, 0)
+    for_both(second_prepare, 2)
+    for_both(second_send, 2)
+    for_both(first_add, 0)
+    for_both(first_send_added, 0)
     take(2)
     take(6)
-    for_both(second_prepare, 2)
-    for_both(second_send, 2)
-    back_message(2, 0)
-    back_message(2, 1)
-    back_send(2, 0)
-    back_send(2, 1)
-    for_both(first_add, 0)
-    for_both(first_send_added, 0)
-    for_both(first_send_plain, 0)
+    for part in (0, 1):
+        back_message(2, part)
+        back_send(2, part)
     for k in (1, 7, 0):
         take(k)
+    back_message(1, 0)
+    back_message(1, 1)
     for s in (1, 3):
         for_both(second_prepare, s)
         for_both(second_send, s)
-    for_both(second_add)
-    for_both(second_send_added)
-    back_message(1, 0)
-    back_message(1, 1)
     back_send(1, 0)
     back_send(1, 1)
     for_both(second_prepare, 0)
@@ -542,9 +533,8 @@
             pltpu.VMEM((2, 4, 6 * QUARTER, W), BF16),
             pltpu.VMEM((2, 4, 2 * QUARTER, W), BF16),
             pltpu.VMEM((2, 4, 4 * QUARTER, W), BF16),
-            pltpu.VMEM((2, 6 * QUARTER, W), BF16),
-            pltpu.VMEM((2, 2 * QUARTER, W), BF16),
-            pltpu.VMEM((2, 4 * QUARTER, W), BF16),
+            pltpu.VMEM((2, 3, HALF, W), BF16),
+            pltpu.VMEM((2, 3, HALF, W), BF16),
             pltpu.VMEM((8, W, ROWS), F32),
             pltpu.VMEM((8, W, ROWS), BF16),
             pltpu.VMEM((8, W, ROWS), BF16),

time: 47.9 us -> 46.8 us (0.977)
  the two profiles are of different devices: /device:TPU:2 before, /device:TPU:1 now
where the time goes in v5:
time: 46.8 us; the launch traced here: 46.7 us
  Pallas kernels  46 us (98%)
  local copies, waits for them, and re-layouts  0.71 us (2%)
    pallas_call x1, Pallas kernels, local(): pl.pallas_call(scoped_kernel, out_shape=jax.ShapeDtypeStruct((ROWS, D), F...  46 us

profile of v5, /device:TPU:1, one launch (start us, length us, event | category | flops | bytes accessed | tf_op | source)
XLA Modules:
  0.0 46.7 jit_solution(1168625254660710478)
XLA Ops:
  0.0 46.0 %shard_map.37 = f32[128,512]{1,0:T(8,128)S(1)} custom-call(f32[128,512]{1,0:T(8,128)} %refs_0_.1, bf16[128,512]{1,0:T(8,128)(2,1)} %refs_1_.1, s32[1,512]{1,0:T(1,128)} %bitcast.1), custom_call_target="tpu_custom_call" | custom-call | tf_op jit(solution)/shard_map/pallas_call | solution.py:509
  46.0 0.7 %copy.5 = f32[128,512]{1,0:T(8,128)} copy(f32[128,512]{1,0:T(8,128)S(1)} %shard_map.37) | data formatting | bytes 524288

commit v6 on v5

--- a/solution.py
+++ b/solution.py
@@ -16,7 +16,7 @@
 HALF = ROWS // 2
 QUARTER = ROWS // 4
 TILE = 4 * HALF
-COPIES = 192
+COPIES = 186
 
 
 def neighbours():
@@ -257,6 +257,10 @@
         rows = targets[half, s, :, 0:W].astype(F32)
         result = product(half, s, slots) + rows * (2.0 * weights[:, :W]) * row_totals
         acc[half, s] = result
+        if s == 2:
+            for n, i in enumerate((2, 1, 3)):
+                sent[half, s, n * HALF : n * HALF + HALF] = result[i * HALF : i * HALF + HALF].astype(BF16)
+            return
         sent[half, s, 0:HALF] = result[2 * HALF : 3 * HALF].astype(BF16)
         sent[half, s, HALF : HALF + QUARTER] = result[HALF + QUARTER : 2 * HALF].astype(BF16)
         sent[half, s, HALF + QUARTER : TILE // 2] = result[3 * HALF : 3 * HALF + QUARTER].astype(BF16)
@@ -285,7 +289,7 @@
         return pl.ds(part * ROWS if step == 1 else (1 - part) * ROWS, ROWS)
 
     def back_message(h, part):
-        came = ([(4, 0), (3, 0)], [(3, 1)])[part] if h == 2 else []
+        came = {(2, 0): [(4, 0), (3, 0)], (2, 1): [(3, 1)], (1, 1): [(2, 1)]}.get((h, part), [])
         for n, step in enumerate((1, -1)):
             value = back[slot(step, h), back_rows(step, part)]
             for at in came:
@@ -299,15 +303,14 @@
                 ("back", h, part, step),
                 back_sent.at[n, h, part],
                 back_came.at[n, h, part],
-                ("z", -step if h % 2 else -2 * step),
+                ("z", -2 * step if part == 0 and h in (2, 4) else -step),
             )
 
     def back_result():
-        for h in (1, 2):
-            for part in (0, 1):
-                for n, step in enumerate((1, -1)):
-                    arrive(("back", h, part, step))
-                    back[0, back_rows(step, part)] += back_came[n, h, part].astype(F32)
+        for h, part in ((1, 0), (2, 0), (1, 1)):
+            for n, step in enumerate((1, -1)):
+                arrive(("back", h, part, step))
+                back[0, back_rows(step, part)] += back_came[n, h, part].astype(F32)
         out_ref[:, W:] = back[0].T
 
     def q4(n):
@@ -316,6 +319,11 @@
     def first_send(half, s):
         axis = axes[half][0]
         base = sent.at[half, s]
+        if s == 2:
+            for n, step in enumerate((2, 1, -1)):
+                rows = pl.ds(n * HALF, HALF)
+                copy(("sum1", half, n), base.at[rows], arrived.at[half, s, rows], (axis, step))
+            return
         copy(("rel", half, s, 1), base.at[q4(0)], relay.at[half, s, q4(0)], (axis, 1))
         copy(("rel", half, s, -1), base.at[q4(1)], relay.at[half, s, q4(1)], (axis, -1))
 
@@ -340,11 +348,16 @@
         copy(("add", half, s, -1), base.at[q4(5)], arrived.at[half, s, q4(3)], (axis, -1))
 
     def first_result(half, s):
+        if s == 2:
+            for n in (1, 2, 0):
+                arrive(("sum1", half, n))
+            came = arrived[half, s].astype(F32)
+            return acc[half, s, pl.ds(0, HALF)] + came[:HALF] + came[HALF : 2 * HALF] + came[2 * HALF :]
         for name in ("pln", "add"):
             for step in (1, -1):
                 arrive((name, half, s, step))
         own = acc[half, s, pl.ds(0, HALF)]
-        came = arrived[half, s].astype(F32)
+        came = arrived[half, s, 0 : 2 * HALF].astype(F32)
         return own + came[:HALF] + came[HALF:]
 
     def second_prepare(half, s):
@@ -415,10 +428,10 @@
     z_step("s", 2)
     t_step3(targets, 2)
     t_step3(target_scores, 0)
+    t_step2(target_scores)
     square_targets(middle)
     make_kernels(middle, (0, 1))
     z_step("r", 3, 0)
-    t_step2(target_scores)
     make_kernels(middle, (7,))
     z_step("r", 3, 1)
     t_step3(target_scores, 3)
@@ -426,75 +439,73 @@
     from_core("r", (2, 6))
     make_kernels(near + middle, (2, 6))
     z_step("s", 3)
+    t_step3(target_scores, 2)
     t_step4(targets)
     square_targets(far)
     make_kernels(far, (0, 1, 7, 2, 6))
     z_step("r", 4)
-    t_step3(target_scores, 2)
     from_core("r", (3, 5))
     make_kernels(every, (3, 5))
     z_step("s", 4)
     from_core("r", (4,))
-    from_core("s", (0, 1, 7, 2, 6, 3, 5))
     make_kernels(every, (4,))
-    slots = (0, 1, 7, 2, 6, 3, 5, 4)
-    from_core("s", (4,))
-    for_both(last_product, 2, slots)
     t_step4(target_scores)
-    for_both(first_send, 2)
-    for_both(first_send_plain, 2)
     turn(every)
     for k in (4, 3, 5):
         back_product(k)
     for k in (4, 3, 5):
         give(k)
+    slots = (0, 1, 7, 2, 6, 3, 5, 4)
+    from_core("s", slots)
     for s in (1, 3):
         for_both(last_product, s, slots)
     for k in (4, 3, 5):
         take(k)
+    back_message(3, 1)
     back_message(4, 0)
     back_message(3, 0)
-    back_message(3, 1)
     for s in (1, 3):
         for_both(first_send, s)
-    for_both(first_add, 2)
+    back_send(3, 1)
     back_send(4, 0)
     back_send(3, 0)
-    back_send(3, 1)
-    for_both(first_send_added, 2)
     for s in (1, 3):
         for_both(first_send_plain, s)
+    for_both(last_product, 2, slots)
+    for_both(first_send, 2)
+    for k in (2, 6):
+        back_product(k)
     for_both(last_product, 0, slots)
     for k in (2, 6):
-        back_product(k)
+        give(k)
     for_both(first_send, 0)
-    for k in (2, 6):
-        give(k)
     for k in (1, 7, 0):
         back_product(k)
     for k in (1, 7, 0):
         give(k)
     for s in (1, 3):
         for_both(first_add, s)
+    for s in (1, 3):
         for_both(first_send_added, s)
     for_both(first_send_plain, 0)
+    take(2)
+    take(6)
+    back_message(2, 1)
+    back_send(2, 1)
+    back_message(2, 0)
+    back_send(2, 0)
+    for_both(first_add, 0)
+    for_both(first_send_added, 0)
     for_both(second_prepare, 2)
     for_both(second_send, 2)
-    for_both(first_add, 0)
-    for_both(first_send_added, 0)
-    take(2)
-    take(6)
-    for part in (0, 1):
-        back_message(2, part)
-        back_send(2, part)
     for k in (1, 7, 0):
         take(k)
     back_message(1, 0)
-    back_message(1, 1)
+    back_send(1, 0)
     for s in (1, 3):
         for_both(second_prepare, s)
         for_both(second_send, s)
-    back_send(1, 0)
+    back_message(1, 1)
     back_send(1, 1)
     for_both(second_prepare, 0)
     for_both(second_result)
@@ -532,7 +543,7 @@
             pltpu.VMEM((W + 16, 8 * TILE), BF16),
             pltpu.VMEM((2, 4, 6 * QUARTER, W), BF16),
             pltpu.VMEM((2, 4, 2 * QUARTER, W), BF16),
-            pltpu.VMEM((2, 4, 4 * QUARTER, W), BF16),
+            pltpu.VMEM((2, 4, 6 * QUARTER, W), BF16),
             pltpu.VMEM((2, 3, HALF, W), BF16),
             pltpu.VMEM((2, 3, HALF, W), BF16),
             pltpu.VMEM((8, W, ROWS), F32),

time: 46.8 us -> 45.4 us (0.970)
  Pallas kernels: 46 us -> 44.5 us
    pallas_call x1, Pallas kernels: 46 us -> 44.5 us  [local(): pl.pallas_call(scoped_kernel, out_shape=jax.ShapeDtypeStruct((ROWS, D), F...]
where the time goes in v6:
time: 45.4 us; the launch traced here: 45.2 us
  Pallas kernels  44.5 us (98%)
  local copies, waits for them, and re-layouts  0.71 us (2%)
    pallas_call x1, Pallas kernels, local(): pl.pallas_call(scoped_kernel, out_shape=jax.ShapeDtypeStruct((ROWS, D), F...  44.5 us

profile of v6, /device:TPU:1, one launch (start us, length us, event | category | flops | bytes accessed | tf_op | source)
XLA Modules:
  0.0 45.2 jit_solution(4368214956482747154)
XLA Ops:
  0.0 44.5 %shard_map.37 = f32[128,512]{1,0:T(8,128)S(1)} custom-call(f32[128,512]{1,0:T(8,128)} %refs_0_.1, bf16[128,512]{1,0:T(8,128)(2,1)} %refs_1_.1, s32[1,512]{1,0:T(1,128)} %bitcast.1), custom_call_target="tpu_custom_call" | custom-call | tf_op jit(solution)/shard_map/pallas_call | solution.py:520
  44.5 0.7 %copy.5 = f32[128,512]{1,0:T(8,128)} copy(f32[128,512]{1,0:T(8,128)S(1)} %shard_map.37) | data formatting | bytes 524288

commit v7 on v6

--- a/solution.py
+++ b/solution.py
@@ -16,7 +16,7 @@
 HALF = ROWS // 2
 QUARTER = ROWS // 4
 TILE = 4 * HALF
-COPIES = 186
+COPIES = 194
 
 
 def neighbours():
@@ -101,8 +101,10 @@
         return h if step == 1 else 8 - h
 
     def piece(size, step, n):
-        first = 0 if step == 1 else 1
-        return pl.ds((first + n) % 2 * (size // 2), size // 2)
+        first = 0 if step == 1 else size // 2
+        if n < 2:
+            return pl.ds(first + n * (size // 4), size // 4)
+        return pl.ds(size // 2 - first, size // 2)
 
     def z_send(kind, h, n):
         for step in (1, -1):
@@ -111,7 +113,7 @@
                 rows = piece(D, step, n)
                 a, b = sources.at[src, 0, rows], sources.at[dst, 0, rows]
             else:
-                rows = piece(ROWS, step, 0) if h == 3 else pl.ds(0, ROWS)
+                rows = pl.ds(0 if step == 1 else HALF, HALF) if h == 3 else pl.ds(0, ROWS)
                 a, b = source_scores.at[src, rows], source_scores.at[dst, rows]
             copy(("z", kind, h + 1, n, step), a, b, ("z", step))
 
@@ -125,9 +127,9 @@
     def z_step(kind, h, n=0):
         for step in (1, -1):
             arrive(("z", kind, h, n, step))
-        if h < 3 or (h == 3 and n == 0):
+        if h < 3 or (h == 3 and n < 2):
             z_send(kind, h, n)
-        if n == 1 or h == 4 or kind == "s":
+        if n == 2 or (h == 4 and n == 1) or kind == "s":
             for s in sorted({h, 8 - h}):
                 to_core(kind, s)
 
@@ -402,6 +404,7 @@
         z_send("r", 0, 0)
         t_start(targets)
         z_send("r", 0, 1)
+        z_send("r", 0, 2)
         to_core("r", 0)
         t_start(target_scores)
         z_send("s", 0, 0)
@@ -412,8 +415,9 @@
     start()
     t_step1(targets)
     z_step("r", 1, 0)
+    z_step("r", 1, 1)
     t_step2(targets)
-    z_step("r", 1, 1)
+    z_step("r", 1, 2)
     from_core("r", (0,))
     t_step3(targets, 0)
     z_step("s", 1)
@@ -422,18 +426,20 @@
     from_core("r", (1, 7))
     make_kernels(near, (0, 1, 7))
     z_step("r", 2, 0)
+    z_step("r", 2, 1)
     t_step3(targets, 3)
-    z_step("r", 2, 1)
+    z_step("r", 2, 2)
     t_step3(targets, 1)
     z_step("s", 2)
     t_step3(targets, 2)
     t_step3(target_scores, 0)
     t_step2(target_scores)
+    z_step("r", 3, 0)
     square_targets(middle)
     make_kernels(middle, (0, 1))
-    z_step("r", 3, 0)
+    z_step("r", 3, 1)
     make_kernels(middle, (7,))
-    z_step("r", 3, 1)
+    z_step("r", 3, 2)
     t_step3(target_scores, 3)
     t_step3(target_scores, 1)
     from_core("r", (2, 6))
@@ -443,7 +449,8 @@
     t_step4(targets)
     square_targets(far)
     make_kernels(far, (0, 1, 7, 2, 6))
-    z_step("r", 4)
+    z_step("r", 4, 0)
+    z_step("r", 4, 1)
     from_core("r", (3, 5))
     make_kernels(every, (3, 5))
     z_step("s", 4)

time: 45.4 us -> 45.1 us (level)
  no operation moved by 1% of the time
where the time goes in v7:
time: 45.1 us; the launch traced here: 45 us
  Pallas kernels  44.3 us (98%)
  local copies, waits for them, and re-layouts  0.71 us (2%)
    pallas_call x1, Pallas kernels, local(): pl.pallas_call(scoped_kernel, out_shape=jax.ShapeDtypeStruct((ROWS, D), F...  44.3 us

profile of v7, /device:TPU:1, one launch (start us, length us, event | category | flops | bytes accessed | tf_op | source)
XLA Modules:
  0.0 45.0 jit_solution(11796387781641038006)
XLA Ops:
  0.0 44.3 %shard_map.37 = f32[128,512]{1,0:T(8,128)S(1)} custom-call(f32[128,512]{1,0:T(8,128)} %refs_0_.1, bf16[128,512]{1,0:T(8,128)(2,1)} %refs_1_.1, s32[1,512]{1,0:T(1,128)} %bitcast.1), custom_call_target="tpu_custom_call" | custom-call | tf_op jit(solution)/shard_map/pallas_call | solution.py:527
  44.3 0.7 %copy.5 = f32[128,512]{1,0:T(8,128)} copy(f32[128,512]{1,0:T(8,128)S(1)} %shard_map.37) | data formatting | bytes 524288

commit v8 on v7

--- a/solution.py
+++ b/solution.py
@@ -90,10 +90,6 @@
     sources[0, 0] = double.T.astype(BF16)
     targets[0, 0, 0:HALF] = rounded[:HALF]
     targets[1, 0, 0:HALF] = rounded[HALF:]
-    folded = (scores[...].astype(F32) - double).astype(BF16)
-    source_scores[0, 0:ROWS] = folded[:, :W]
-    target_scores[0, 0, 0:HALF] = folded[:HALF, W:]
-    target_scores[1, 0, 0:HALF] = folded[HALF:, W:]
 
     pl.semaphore_wait(barrier, len(ids))
 
@@ -406,11 +402,15 @@
         z_send("r", 0, 1)
         z_send("r", 0, 2)
         to_core("r", 0)
+        folded = (scores[...].astype(F32) - double).astype(BF16)
+        source_scores[0, 0:ROWS] = folded[:, :W]
+        target_scores[0, 0, 0:HALF] = folded[:HALF, W:]
+        target_scores[1, 0, 0:HALF] = folded[HALF:, W:]
+        inverse[...] = jnp.broadcast_to(0.25 / weights, (ROWS, D)).T
+        turned[W:] = jnp.ones((16, 8 * TILE), BF16)
         t_start(target_scores)
         z_send("s", 0, 0)
         to_core("s", 0)
-        inverse[...] = jnp.broadcast_to(0.25 / weights, (ROWS, D)).T
-        turned[W:] = jnp.ones((16, 8 * TILE), BF16)
 
     start()
     t_step1(targets)
@@ -453,11 +453,12 @@
     z_step("r", 4, 1)
     from_core("r", (3, 5))
     make_kernels(every, (3, 5))
+    turn(near + middle)
     z_step("s", 4)
     from_core("r", (4,))
     make_kernels(every, (4,))
     t_step4(target_scores)
-    turn(every)
+    turn(far)
     for k in (4, 3, 5):
         back_product(k)
     for k in (4, 3, 5):
@@ -512,14 +513,18 @@
     for s in (1, 3):
         for_both(second_prepare, s)
         for_both(second_send, s)
+    gathers = [name for name in copies if name[0] in ("z", "core", "c1", "c2", "c3", "c6", "give")]
+    for name in gathers:
+        copies[name].wait_send()
     back_message(1, 1)
     back_send(1, 1)
     for_both(second_prepare, 0)
     for_both(second_result)
     back_result()
 
-    for made in copies.values():
-        made.wait_send()
+    for name, made in copies.items():
+        if name not in gathers:
+            made.wait_send()
     assert len(copies) <= COPIES
 
 

time: 45.1 us -> 44.9 us (level)
  no operation moved by 1% of the time
where the time goes in v8:
time: 44.9 us; the launch traced here: 44.7 us
  Pallas kernels  44 us (98%)
  local copies, waits for them, and re-layouts  0.71 us (2%)
    pallas_call x1, Pallas kernels, local(): pl.pallas_call(scoped_kernel, out_shape=jax.ShapeDtypeStruct((ROWS, D), F...  44 us

profile of v8, /device:TPU:1, one launch (start us, length us, event | category | flops | bytes accessed | tf_op | source)
XLA Modules:
  0.0 44.7 jit_solution(6650848013784537980)
XLA Ops:
  0.0 44.0 %shard_map.37 = f32[128,512]{1,0:T(8,128)S(1)} custom-call(f32[128,512]{1,0:T(8,128)} %refs_0_.1, bf16[128,512]{1,0:T(8,128)(2,1)} %refs_1_.1, s32[1,512]{1,0:T(1,128)} %bitcast.1), custom_call_target="tpu_custom_call" | custom-call | tf_op jit(solution)/shard_map/pallas_call | solution.py:532
  44.0 0.7 %copy.5 = f32[128,512]{1,0:T(8,128)} copy(f32[128,512]{1,0:T(8,128)S(1)} %shard_map.37) | data formatting | bytes 524288
